TPU v7x, 128 devices: a whole 4x4x4 slice. The times are simulated.
128 devices in a mesh: img: 1, cfg: 2 (over core), patch: 64 (over z, y, x).
Axes of the slice: x: 4, y: 4, z: 4, core: 2. Of those that a mesh axis runs over, the one named last changes fastest.
Arguments:
- latent: bfloat16 [1, 2048, 3072], P('img', 'patch')
- cond_vec: float32 [2, 2, 3072], P(('img', 'cfg'))
- sched_coef: float32 [3, 2], replicated
- w_ada: bfloat16 [2, 3072, 18432], replicated
- w_qkv: bfloat16 [2, 3072, 9216], replicated
- w_out: bfloat16 [2, 24, 128, 3072], replicated
- w_up: bfloat16 [2, 3072, 12288], replicated
- w_down: bfloat16 [2, 12288, 3072], replicated
- w_head: bfloat16 [3072, 3072], replicated
- k_stale: bfloat16 [2, 2, 2048, 3072], P(('img', 'cfg'))
- v_stale: bfloat16 [2, 2, 2048, 3072], P(('img', 'cfg'))
Outputs:
- output 1: float32 [2, 2048, 3072], P(('img', 'cfg'), 'patch')
- output 2: bfloat16 [2, 2, 2048, 3072], P(('img', 'cfg'))
- output 3: bfloat16 [2, 2, 2048, 3072], P(('img', 'cfg'))
All inputs are finite; a program needn't handle non-finite values.
Results may differ from a plain program's by a relative error of at most 0.0132624.
Values are sent between devices in bfloat16 or wider.
A program may use at most 1.5 GiB of HBM per device.

v0:
```python
import jax
import jax.numpy as jnp
from jax import lax
from jax.sharding import PartitionSpec as P


def layer_norm(values):
    row_mean = jnp.mean(values, -1, keepdims=True)
    centered = values - row_mean
    row_var = jnp.mean(centered * centered, -1, keepdims=True)
    return centered * lax.rsqrt(row_var + 1e-6)


def attend(queries, key_set, value_set, n_heads, head_dim):
    local_rows = queries.shape[0]
    tokens = key_set.shape[0]
    q_blk = min(local_rows, 128)
    blocks = queries.reshape(local_rows // q_blk, q_blk, n_heads, head_dim)
    key_h = key_set.reshape(tokens, n_heads, head_dim)
    val_h = value_set.reshape(tokens, n_heads, head_dim)
    score_scale = head_dim ** -0.5

    def one_block(q_part):
        scores = jnp.einsum("qhe,khe->hqk", q_part, key_h, preferred_element_type=jnp.float32) * score_scale
        row_max = jnp.max(scores, -1, keepdims=True)
        weights = jnp.exp(scores - row_max)
        row_sum = jnp.sum(weights, -1)
        mixed_out = jnp.einsum("hqk,khe->qhe", weights.astype(jnp.bfloat16), val_h, preferred_element_type=jnp.float32)
        return (mixed_out / row_sum.T[:, :, None]).astype(jnp.bfloat16)

    return lax.map(one_block, blocks).reshape(local_rows, n_heads, head_dim)


def solution(mesh):
    n_cfg = mesh.shape["cfg"]
    partner = [(dev_pos, dev_pos ^ 1) for dev_pos in range(n_cfg)]
    slot_spec = P(("img", "cfg"), None, None)
    cache_spec = P(("img", "cfg"), None, None, None)
    rep_spec = P()

    def local_step(latent, cond_vec, sched_coef, w_ada, w_qkv, w_out, w_up, w_down, w_head, k_stale, v_stale):
        n_layers = k_stale.shape[1]
        local_rows = latent.shape[1]
        n_heads = w_out.shape[1]
        head_dim = w_out.shape[2]
        cfg_slot = lax.axis_index("cfg")
        row_start = lax.axis_index("patch") * local_rows
        is_cond = cfg_slot % 2 == 0
        latent_now = lax.dynamic_index_in_dim(latent, cfg_slot // 2, axis=0, keepdims=False).astype(jnp.float32)
        mod_all = jnp.einsum("td,lde->tle", jax.nn.silu(cond_vec[0]).astype(jnp.bfloat16), w_ada, preferred_element_type=jnp.float32)
        k_cache = [k_stale[0, layer_idx] for layer_idx in range(n_layers)]
        v_cache = [v_stale[0, layer_idx] for layer_idx in range(n_layers)]
        for step_idx in range(sched_coef.shape[1]):
            resid_now = latent_now
            k_next = []
            v_next = []
            for layer_idx in range(n_layers):
                shift_attn, scale_attn, gate_attn, shift_mlp, scale_mlp, gate_mlp = jnp.split(mod_all[step_idx, layer_idx], 6)
                norm_attn = (layer_norm(resid_now) * (1.0 + scale_attn) + shift_attn).astype(jnp.bfloat16)
                qkv_all = jnp.dot(norm_attn, w_qkv[layer_idx], preferred_element_type=jnp.float32).astype(jnp.bfloat16)
                q_new, k_new, v_new = jnp.split(qkv_all, 3, axis=-1)
                k_next.append(lax.all_gather(k_new, "patch", axis=0, tiled=True))
                v_next.append(lax.all_gather(v_new, "patch", axis=0, tiled=True))
                key_set = lax.dynamic_update_slice(k_cache[layer_idx], k_new, (row_start, 0))
                value_set = lax.dynamic_update_slice(v_cache[layer_idx], v_new, (row_start, 0))
                heads_out = attend(q_new, key_set, value_set, n_heads, head_dim)
                attn_out = jnp.einsum("qhe,hed->qd", heads_out, w_out[layer_idx], preferred_element_type=jnp.float32)
                resid_now = resid_now + gate_attn * attn_out
                norm_mlp = (layer_norm(resid_now) * (1.0 + scale_mlp) + shift_mlp).astype(jnp.bfloat16)
                mlp_up = jnp.dot(norm_mlp, w_up[layer_idx], preferred_element_type=jnp.float32)
                mlp_act = jax.nn.gelu(mlp_up, approximate=True).astype(jnp.bfloat16)
                mlp_down = jnp.dot(mlp_act, w_down[layer_idx], preferred_element_type=jnp.float32)
                resid_now = resid_now + gate_mlp * mlp_down
            k_cache = k_next
            v_cache = v_next
            eps_own = jnp.dot(layer_norm(resid_now).astype(jnp.bfloat16), w_head, preferred_element_type=jnp.float32).astype(jnp.bfloat16)
            eps_peer = lax.ppermute(eps_own, "cfg", partner)
            eps_cond = jnp.where(is_cond, eps_own, eps_peer).astype(jnp.float32)
            eps_unc = jnp.where(is_cond, eps_peer, eps_own).astype(jnp.float32)
            guided = eps_unc + sched_coef[2, step_idx] * (eps_cond - eps_unc)
            latent_now = sched_coef[0, step_idx] * latent_now + sched_coef[1, step_idx] * guided
        return latent_now[None], jnp.stack(k_cache)[None], jnp.stack(v_cache)[None]

    return jax.shard_map(
        local_step,
        mesh=mesh,
        in_specs=(P("img", "patch", None), slot_spec, rep_spec, rep_spec, rep_spec, rep_spec, rep_spec, rep_spec, rep_spec, cache_spec, cache_spec),
        out_specs=(P(("img", "cfg"), "patch", None), cache_spec, cache_spec),
        check_vma=False,
    )
```

profile of v0, /device:TPU:1, one launch (start us, length us, event | category | flops | bytes accessed | tf_op | source)
XLA Modules:
  0.0 906.2 jit_solution(15635274608802314972)
XLA Ops:
  7.2 69.9 %fusion.356 = f32[2,2,18432]{2,0,1:T(2,128)S(1)} fusion(bf16[2,3072,18432]{2,1,0:T(8,128)(2,1)} %param.14, f32[1,2,3072]{2,1,0:T(2,128)} %param.12), kind=kOutput, calls=%fused_computation.290 | convolution fusion | flops 453015552 | bytes 226811904 | tf_op jit(solution)/shard_map/td,lde->tle/dot_general | solution.py:50
  77.6 33.9 %slice_bitcast_fusion = (bf16[2048,3072]{1,0:T(8,128)(2,1)}, bf16[2048,3072]{1,0:T(8,128)(2,1)}, bf16[2048,3072]{1,0:T(8,128)(2,1)}, bf16[2048,3072]{1,0:T(8,128)(2,1)}) fusion(bf16[1,2,2048,3072]{3,2,1,0:T(8,128)(2,1)} %param.20, bf16[1,2,2048,3072]{3,2,1,0:T(8,128)(2,1)} %param.21), kind=kLoop, calls=%fused_computation.62 | loop fusion | bytes 100663296 | tf_op jit(solution)/shard_map/squeeze | solution.py:51
  111.5 20.9 %fusion.60 = bf16[32,9216]{1,0:T(8,128)(2,1)S(1)} fusion(bf16[2,3072,9216]{2,1,0:T(8,128)(2,1)} %param.15, bf16[1,32,3072]{2,1,0:T(8,128)(2,1)S(1)} %copy-done.6, f32[3072]{0:T(1024)S(1)} %bitcast.420, f32[3072]{0:T(1024)S(1)} %bitcast.421, f32[32]{0:T(128)S(1)} %add_rsqrt_fusion.9, f32[32]{0:T(128)S(1)} %broadcast_multiply_fusion.9), kind=kOutput, calls=%fused_computation.66 | convolution fusion | flops 1812824064 | bytes 57434368 | tf_op jit(solution)/shard_map/dot_general | solution.py:60
  134.3 16.6 %copy.26 = bf16[2048,3072]{0,1:T(8,128)(2,1)} copy(bf16[2048,3072]{1,0:T(8,128)(2,1)} %get-tuple-element.85) | data formatting | bytes 25165824 | tf_op jit(solution)/shard_map/reshape | solution.py:20
  178.3 26.8 %fusion.165.clone.1.clone.5 = bf16[32,12288]{1,0:T(8,128)(2,1)S(1)} fusion(bf16[2,3072,12288]{2,1,0:T(8,128)(2,1)} %param.17, f32[32,3072]{1,0:T(8,128)S(1)} %get-tuple-element.122, f32[3072]{0:T(1024)S(1)} %bitcast.422, f32[3072]{0:T(1024)S(1)} %bitcast.412, f32[32]{0:T(128)S(1)} %add_rsqrt_fusion.8, ...), kind=kOutput, calls=%fused_computation.131.clone.clone.clone.clone.clone.2 | convolution fusion | flops 2419949568 | bytes 76701952 | tf_op jit(solution)/shard_map/dot_general | solution.py:70
  205.1 26.3 %fusion.396 = (f32[32]{0:T(128)S(1)}, f32[32,3072]{1,0:T(8,128)S(1)}) fusion(f32[32,3072]{1,0:T(8,128)S(1)} %get-tuple-element.122, bf16[2,12288,3072]{2,1,0:T(8,128)(2,1)} %param.18, f32[3072]{0:T(1024)S(1)} %bitcast.411, bf16[32,12288]{1,0:T(8,128)(2,1)S(1)} %fusion.165.clone.1.clone.5), kind=kOutput, calls=%fused_computation.350 | convolution fusion | flops 2416214016 | bytes 77082752 | tf_op jit(solution)/shard_map/dot_general | solution.py:72
  231.6 21.3 %fusion.66 = bf16[32,9216]{1,0:T(8,128)(2,1)S(1)} fusion(bf16[2,3072,9216]{2,1,0:T(8,128)(2,1)} %param.15, f32[32,3072]{1,0:T(8,128)S(1)} %get-tuple-element.124, f32[3072]{0:T(1024)S(1)} %bitcast.418, f32[3072]{0:T(1024)S(1)} %bitcast.419, f32[32]{0:T(128)S(1)} %add_rsqrt_fusion.7, f32[32]{0:T(128)S(1)} %broadcast_multiply_fusion.7), kind=kOutput, calls=%fused_computation.68 | convolution fusion | flops 1812725760 | bytes 57630976 | tf_op jit(solution)/shard_map/dot_general | solution.py:60
  254.5 16.6 %copy.27 = bf16[2048,3072]{0,1:T(8,128)(2,1)} copy(bf16[2048,3072]{1,0:T(8,128)(2,1)} %get-tuple-element.80) | data formatting | bytes 25165824 | tf_op jit(solution)/shard_map/reshape | solution.py:20
  297.6 26.8 %fusion.179.clone.1.clone.5 = bf16[32,12288]{1,0:T(8,128)(2,1)S(1)} fusion(bf16[2,3072,12288]{2,1,0:T(8,128)(2,1)} %param.17, f32[32,3072]{1,0:T(8,128)S(1)} %get-tuple-element.128, f32[3072]{0:T(1024)S(1)} %bitcast.414, f32[3072]{0:T(1024)S(1)} %bitcast.415, f32[32]{0:T(128)S(1)} %add_rsqrt_fusion.6, ...), kind=kOutput, calls=%fused_computation.139.clone.clone.clone.clone.clone.2 | convolution fusion | flops 2419949568 | bytes 76701952 | tf_op jit(solution)/shard_map/dot_general | solution.py:70
  324.5 26.5 %fusion.402 = (f32[32]{0:T(128)S(1)}, f32[32,3072]{1,0:T(8,128)S(1)}) fusion(f32[32,3072]{1,0:T(8,128)S(1)} %get-tuple-element.128, bf16[2,12288,3072]{2,1,0:T(8,128)(2,1)} %param.18, f32[3072]{0:T(1024)S(1)} %bitcast.413, bf16[32,12288]{1,0:T(8,128)(2,1)S(1)} %fusion.179.clone.1.clone.5), kind=kOutput, calls=%fused_computation.352 | convolution fusion | flops 2416214016 | bytes 77082752 | tf_op jit(solution)/shard_map/dot_general | solution.py:72
  366.0 20.8 %fusion.63 = bf16[32,9216]{1,0:T(8,128)(2,1)S(1)} fusion(bf16[2,3072,9216]{2,1,0:T(8,128)(2,1)} %param.15, f32[32,3072]{1,0:T(8,128)S(1)} %get-tuple-element.44, f32[3072]{0:T(1024)S(1)} %bitcast.409, f32[3072]{0:T(1024)S(1)} %bitcast.410, f32[32]{0:T(128)S(1)} %add_rsqrt_fusion.4, f32[32]{0:T(128)S(1)} %broadcast_multiply_fusion.4), kind=kOutput, calls=%fused_computation.67 | convolution fusion | flops 1812725760 | bytes 57630976 | tf_op jit(solution)/shard_map/dot_general | solution.py:60
  387.8 16.6 %copy.28 = bf16[2048,3072]{0,1:T(8,128)(2,1)} copy(bf16[2048,3072]{1,0:T(8,128)(2,1)} %get-tuple-element.60) | data formatting | bytes 25165824 | tf_op jit(solution)/shard_map/reshape | solution.py:20
  431.1 26.8 %fusion.193.clone.1.clone.2 = bf16[32,12288]{1,0:T(8,128)(2,1)S(1)} fusion(bf16[2,3072,12288]{2,1,0:T(8,128)(2,1)} %param.17, f32[32,3072]{1,0:T(8,128)S(1)} %get-tuple-element.134, f32[3072]{0:T(1024)S(1)} %bitcast.406, f32[3072]{0:T(1024)S(1)} %bitcast.407, f32[32]{0:T(128)S(1)} %add_rsqrt_fusion.3, ...), kind=kOutput, calls=%fused_computation.147.clone.clone.clone.clone.clone | convolution fusion | flops 2419949568 | bytes 76701952 | tf_op jit(solution)/shard_map/dot_general | solution.py:70
  457.9 26.5 %fusion.408 = (f32[32]{0:T(128)S(1)}, f32[32,3072]{1,0:T(8,128)S(1)}) fusion(f32[32,3072]{1,0:T(8,128)S(1)} %get-tuple-element.134, bf16[2,12288,3072]{2,1,0:T(8,128)(2,1)} %param.18, f32[3072]{0:T(1024)S(1)} %bitcast.405, bf16[32,12288]{1,0:T(8,128)(2,1)S(1)} %fusion.193.clone.1.clone.2), kind=kOutput, calls=%fused_computation.354 | convolution fusion | flops 2416214016 | bytes 77082752 | tf_op jit(solution)/shard_map/dot_general | solution.py:72
  484.7 20.8 %fusion.69 = bf16[32,9216]{1,0:T(8,128)(2,1)S(1)} fusion(bf16[2,3072,9216]{2,1,0:T(8,128)(2,1)} %param.15, f32[32,3072]{1,0:T(8,128)S(1)} %get-tuple-element.136, f32[3072]{0:T(1024)S(1)} %bitcast.403, f32[3072]{0:T(1024)S(1)} %bitcast.404, f32[32]{0:T(128)S(1)} %add_rsqrt_fusion.2, f32[32]{0:T(128)S(1)} %broadcast_multiply_fusion.2), kind=kOutput, calls=%fused_computation.69 | convolution fusion | flops 1812725760 | bytes 57630976 | tf_op jit(solution)/shard_map/dot_general | solution.py:60
  509.4 16.6 %copy.29 = bf16[2048,3072]{0,1:T(8,128)(2,1)} copy(bf16[2048,3072]{1,0:T(8,128)(2,1)} %get-tuple-element.70) | data formatting | bytes 25165824 | tf_op jit(solution)/shard_map/reshape | solution.py:20
  537.4 15.0 %fusion.411 = (f32[32]{0:T(128)S(1)}, f32[32,3072]{1,0:T(8,128)S(1)}) fusion(f32[32,3072]{1,0:T(8,128)S(1)} %get-tuple-element.136, bf16[2,24,128,3072]{3,2,1,0:T(8,128)(2,1)} %param.16, bf16[2048,24,128]{0,2,1:T(8,128)(2,1)} %bitcast.388, f32[24,32,2048]{2,1,0:T(8,128)} %copy-done.1, f32[24,32]{1,0:T(8,128)S(1)} %get-tuple-element.137, ...), kind=kOutput, calls=%fused_computation.355 | convolution fusion | flops 1011843072 | bytes 38553728 | tf_op jit(solution)/shard_map/qhe,hed->qd/dot_general | solution.py:67
  552.7 26.8 %fusion.207.clone.1.clone.2 = bf16[32,12288]{1,0:T(8,128)(2,1)S(1)} fusion(bf16[2,3072,12288]{2,1,0:T(8,128)(2,1)} %param.17, f32[32,3072]{1,0:T(8,128)S(1)} %get-tuple-element.140, f32[3072]{0:T(1024)S(1)} %bitcast.400, f32[3072]{0:T(1024)S(1)} %bitcast.401, f32[32]{0:T(128)S(1)} %add_rsqrt_fusion.1, ...), kind=kOutput, calls=%fused_computation.155.clone.clone.clone.clone.clone | convolution fusion | flops 2419949568 | bytes 76701952 | tf_op jit(solution)/shard_map/dot_general | solution.py:70
  579.5 26.5 %fusion.414 = (f32[32]{0:T(128)S(1)}, f32[32,3072]{1,0:T(8,128)S(1)}) fusion(f32[32,3072]{1,0:T(8,128)S(1)} %get-tuple-element.140, bf16[2,12288,3072]{2,1,0:T(8,128)(2,1)} %param.18, f32[3072]{0:T(1024)S(1)} %bitcast.399, bf16[32,12288]{1,0:T(8,128)(2,1)S(1)} %fusion.207.clone.1.clone.2), kind=kOutput, calls=%fused_computation.356 | convolution fusion | flops 2416214016 | bytes 77082752 | tf_op jit(solution)/shard_map/dot_general | solution.py:72
  620.9 71.4 %all-gather.17.cloned.1.call-done = bf16[2048,3072]{1,0:T(8,128)(2,1)} async-done(((bf16[32,3072]{1,0:T(8,128)(2,1)}), bf16[2048,3072]{1,0:T(8,128)(2,1)}) %all-gather.17.cloned.1.call-update) | async-done | bytes 12582928 | tf_op jit(solution)/shard_map/all_gather | solution.py:62
  692.3 20.5 %maximum_bitcast_fusion = bf16[1,2,2048,3072]{3,2,1,0:T(8,128)(2,1)} fusion(bf16[1,2048,3072]{2,1,0:T(8,128)(2,1)} %bitcast.391, bf16[1,2048,3072]{2,1,0:T(8,128)(2,1)} %bitcast.392), kind=kLoop, calls=%fused_computation.36 | loop fusion | flops 12582912 | bytes 50331648 | tf_op jit(solution)/shard_map/broadcast_in_dim | solution.py:82
  712.8 72.5 %all-gather.23.cloned.1.call-done = bf16[2048,3072]{1,0:T(8,128)(2,1)} async-done(((bf16[32,3072]{1,0:T(8,128)(2,1)}), bf16[2048,3072]{1,0:T(8,128)(2,1)}) %all-gather.23.cloned.1.call-update) | async-done | bytes 12582928 | tf_op jit(solution)/shard_map/all_gather | solution.py:63
  785.3 93.1 %all-gather.21.cloned.1.call-done = bf16[2048,3072]{1,0:T(8,128)(2,1)} async-done(((bf16[32,3072]{1,0:T(8,128)(2,1)}), bf16[2048,3072]{1,0:T(8,128)(2,1)}) %all-gather.21.cloned.1.call-update) | async-done | bytes 12582928 | tf_op jit(solution)/shard_map/all_gather | solution.py:63
  878.4 20.5 %maximum_bitcast_fusion.1 = bf16[1,2,2048,3072]{3,2,1,0:T(8,128)(2,1)} fusion(bf16[1,2048,3072]{2,1,0:T(8,128)(2,1)} %bitcast.393, bf16[1,2048,3072]{2,1,0:T(8,128)(2,1)} %bitcast.394), kind=kLoop, calls=%fused_computation.37 | loop fusion | flops 12582912 | bytes 50331648 | tf_op jit(solution)/shard_map/broadcast_in_dim | solution.py:82
  (120 shorter events, 131.4 us)
Async XLA Ops:
  7.2 379.7 %all-gather.9.cloned.1.call-start = ((), (), s32[]{:S(2)}) async-start(), calls=%async_computation | async-start | bytes 12779520 | tf_op jit(solution)/shard_map/all_gather | solution.py:63
  7.2 69.9 %copy-start.6 = (bf16[1,32,3072]{2,1,0:T(8,128)(2,1)S(1)}, bf16[1,32,3072]{2,1,0:T(8,128)(2,1)}, u32[]{:S(2)}) copy-start(bf16[1,32,3072]{2,1,0:T(8,128)(2,1)} %param.11) | copy-start | bytes 589828
  133.3 253.6 %all-gather.11.cloned.1.call-start = ((), (), s32[]{:S(2)}) async-start(), calls=%async_computation.1 | async-start | bytes 12779520 | tf_op jit(solution)/shard_map/all_gather | solution.py:62
  134.0 371.5 %all-gather.13.cloned.1.call-start = ((), (), s32[]{:S(2)}) async-start(), calls=%async_computation.2 | async-start | bytes 12779520 | tf_op jit(solution)/shard_map/all_gather | solution.py:63
  253.8 252.6 %all-gather.15.cloned.1.call-start = ((), (), s32[]{:S(2)}) async-start(), calls=%async_computation.3 | async-start | bytes 12779520 | tf_op jit(solution)/shard_map/all_gather | solution.py:62
  254.4 366.5 %all-gather.19.cloned.1.call-start = ((), (), s32[]{:S(2)}) async-start(), calls=%async_computation.5 | async-start | bytes 12779520 | tf_op jit(solution)/shard_map/all_gather | solution.py:62
  351.2 12.4 %copy-start.7 = (bf16[1,32,3072]{2,1,0:T(8,128)(2,1)S(1)}, bf16[1,32,3072]{2,1,0:T(8,128)(2,1)}, u32[]{:S(2)}) copy-start(bf16[1,32,3072]{2,1,0:T(8,128)(2,1)} %param.11) | copy-start | bytes 589828
  351.2 14.8 %copy-start.18 = (f32[1,1,3072]{2,0,1:T(1,128)S(1)}, f32[1,1,3072]{2,0,1:T(1,128)}, u32[]{:S(2)}) copy-start(f32[1,1,3072]{2,0,1:T(1,128)} %get-tuple-element.98) | copy-start | bytes 36868
  351.2 14.8 %copy-start.19 = (f32[1,1,3072]{2,0,1:T(1,128)S(1)}, f32[1,1,3072]{2,0,1:T(1,128)}, u32[]{:S(2)}) copy-start(f32[1,1,3072]{2,0,1:T(1,128)} %get-tuple-element.99) | copy-start | bytes 36868
  361.0 2.5 collective-permute-start
  365.7 50.0 %copy-start.4 = (f32[32,3072]{1,0:T(8,128)}, f32[32,3072]{1,0:T(8,128)S(1)}, u32[]{:S(2)}) copy-start(f32[32,3072]{1,0:T(8,128)S(1)} %get-tuple-element.44) | copy-start | bytes 1179652
  415.8 15.3 %copy-start.15 = (f32[1,1,3072]{2,0,1:T(1,128)S(1)}, f32[1,1,3072]{2,0,1:T(1,128)}, u32[]{:S(2)}) copy-start(f32[1,1,3072]{2,0,1:T(1,128)} %get-tuple-element.95) | copy-start | bytes 36868
  415.8 15.3 %copy-start.16 = (f32[1,1,3072]{2,0,1:T(1,128)S(1)}, f32[1,1,3072]{2,0,1:T(1,128)}, u32[]{:S(2)}) copy-start(f32[1,1,3072]{2,0,1:T(1,128)} %get-tuple-element.96) | copy-start | bytes 36868
  431.1 26.8 %copy-start.14 = (f32[1,1,3072]{2,0,1:T(1,128)S(1)}, f32[1,1,3072]{2,0,1:T(1,128)}, u32[]{:S(2)}) copy-start(f32[1,1,3072]{2,0,1:T(1,128)} %get-tuple-element.97) | copy-start | bytes 36868
  457.9 26.8 %copy-start.12 = (f32[1,1,3072]{2,0,1:T(1,128)S(1)}, f32[1,1,3072]{2,0,1:T(1,128)}, u32[]{:S(2)}) copy-start(f32[1,1,3072]{2,0,1:T(1,128)} %get-tuple-element.92) | copy-start | bytes 36868
  457.9 26.8 %copy-start.13 = (f32[1,1,3072]{2,0,1:T(1,128)S(1)}, f32[1,1,3072]{2,0,1:T(1,128)}, u32[]{:S(2)}) copy-start(f32[1,1,3072]{2,0,1:T(1,128)} %get-tuple-element.93) | copy-start | bytes 36868
  507.3 184.9 %all-gather.17.cloned.1.call-start = ((), (), s32[]{:S(2)}) async-start(), calls=%async_computation.4 | async-start | bytes 12779520 | tf_op jit(solution)/shard_map/all_gather | solution.py:62
  507.9 277.4 %all-gather.23.cloned.1.call-start = ((), (), s32[]{:S(2)}) async-start(), calls=%async_computation.7 | async-start | bytes 12779520 | tf_op jit(solution)/shard_map/all_gather | solution.py:63
  508.7 369.7 %all-gather.21.cloned.1.call-start = ((), (), s32[]{:S(2)}) async-start(), calls=%async_computation.6 | async-start | bytes 12779520 | tf_op jit(solution)/shard_map/all_gather | solution.py:63
  537.4 15.3 %copy-start.9 = (f32[1,1,3072]{2,0,1:T(1,128)S(1)}, f32[1,1,3072]{2,0,1:T(1,128)}, u32[]{:S(2)}) copy-start(f32[1,1,3072]{2,0,1:T(1,128)} %get-tuple-element.90) | copy-start | bytes 36868
  537.4 15.3 %copy-start.10 = (f32[1,1,3072]{2,0,1:T(1,128)S(1)}, f32[1,1,3072]{2,0,1:T(1,128)}, u32[]{:S(2)}) copy-start(f32[1,1,3072]{2,0,1:T(1,128)} %get-tuple-element.91) | copy-start | bytes 36868
  552.7 26.8 %copy-start.8 = (f32[1,1,3072]{2,0,1:T(1,128)S(1)}, f32[1,1,3072]{2,0,1:T(1,128)}, u32[]{:S(2)}) copy-start(f32[1,1,3072]{2,0,1:T(1,128)} %get-tuple-element.89) | copy-start | bytes 36868
  606.3 11.9 %copy-start.5 = (f32[32,3072]{1,0:T(8,128)S(1)}, f32[32,3072]{1,0:T(8,128)}, u32[]{:S(2)}) copy-start(f32[32,3072]{1,0:T(8,128)} %copy-done.4) | copy-start | bytes 1179652
  616.1 2.1 collective-permute-start.1
  (7 other events, 44.8 us)
Sparse Core Ops, SparseCore 0:
  133.4 93.6 all-gather.8
  229.9 90.2 all-gather.10
  323.0 90.4 all-gather.12
  416.1 90.2 all-gather.14
  509.0 90.2 all-gather.18
  602.0 90.2 all-gather.16
  695.0 90.2 all-gather.22
  788.1 90.2 all-gather.20
where the time goes:
time: 914 us; the launch traced here: 906 us
  matrix products  476 us (52%)
  waiting for transfers between devices  243 us (27%)
  local copies, waits for them, and re-layouts  116 us (13%)
  other arithmetic  54.2 us (6%)
  between operations  14.9 us (2%)
    all_gather x4, waiting for transfers between devices, local_step(): v_next.append(lax.all_gather(v_new, 'patch', axis=0, tiled=True))  166 us
    dot_general x4, matrix products, local_step(): jnp.dot(norm_mlp, w_up[layer_idx], preferred_element_type=jnp.float32)  107 us
    dot_general x4, matrix products, local_step(): jnp.dot(mlp_act, w_down[layer_idx], preferred_element_type=jnp.float32)  106 us
    dot_general x4, matrix products, local_step(): jnp.dot(norm_attn, w_qkv[layer_idx], preferred_element_type=jnp.float32)  83.7 us
    all_gather x4, waiting for transfers between devices, local_step(): k_next.append(lax.all_gather(k_new, 'patch', axis=0, tiled=True))  72.3 us
    dot_general x1, matrix products, local_step(): jnp.einsum('td,lde->tle', jax.nn.silu(cond_vec[0]).astype(jnp.bfloat16),...  69.9 us
    reshape x4, local copies, waits for them, and re-layouts, attend(): val_h = value_set.reshape(tokens, n_heads, head_dim)  66.4 us
    dot_general x4, matrix products, local_step(): jnp.einsum('qhe,hed->qd', heads_out, w_out[layer_idx], preferred_element_...  60 us
  transfers between devices with their start and end apart: 10, of which 6 were waited for; matrix products, arithmetic and copies ran while one was open for 54% of the time, Pallas kernels for 0%

commit v1 on v0

--- a/solution.py
+++ b/solution.py
@@ -1,7 +1,14 @@
 import jax
 import jax.numpy as jnp
 from jax import lax
+from jax.experimental import pallas as pl
+from jax.experimental.pallas import tpu as pltpu
 from jax.sharding import PartitionSpec as P
+
+RING = 4
+AXES = ("z", "y", "x")
+COLOR_ORDERS = (("x", "y", "z"), ("y", "z", "x"), ("z", "x", "y"))
+MESH = pl.DeviceIdType.MESH
 
 
 def layer_norm(values):
@@ -31,6 +38,128 @@
     return lax.map(one_block, blocks).reshape(local_rows, n_heads, head_dim)
 
 
+def torus_position():
+    patch = lax.axis_index("patch")
+    return {"z": patch // (RING * RING), "y": (patch // RING) % RING, "x": patch % RING}
+
+
+def patch_at(pos):
+    return (pos["z"] * RING + pos["y"]) * RING + pos["x"]
+
+
+def shifted(pos, axis, by):
+    return {**pos, axis: lax.rem(pos[axis] + (by % RING), RING)}
+
+
+def device_of(pos):
+    return {"patch": patch_at(pos)}
+
+
+def ring_copies(ref, color, stage, pos, send_sem, recv_sem):
+    order = COLOR_ORDERS[color]
+    axis = order[stage]
+    width = ref.shape[4] // 3
+    base = color * width
+    half = width // 2
+
+    def region(coord, start, size):
+        index = []
+        for name in AXES:
+            if name == axis:
+                index.append(coord)
+            elif name in order[:stage]:
+                index.append(slice(None))
+            else:
+                index.append(pos[name])
+        return ref.at[(*index, slice(None), pl.ds(start, size))]
+
+    def copy(coord, start, size, to, slot):
+        part = region(coord, start, size)
+        return pltpu.make_async_remote_copy(
+            src_ref=part,
+            dst_ref=part,
+            send_sem=send_sem.at[slot],
+            recv_sem=recv_sem.at[slot],
+            device_id=device_of(shifted(pos, axis, to)),
+            device_id_type=MESH,
+        )
+
+    me = pos[axis]
+    prev = lax.rem(me + RING - 1, RING)
+    succ = lax.rem(me + 1, RING)
+    return (
+        copy(me, base, width, 1, 0),
+        copy(me, base, width, -1, 1),
+        copy(prev, base, half, 1, 2),
+        copy(succ, base + half, half, -1, 3),
+    )
+
+
+def gather_kernel(own_k, own_v, all_k, all_v, local_sem, send_sem, recv_sem):
+    pos = torus_position()
+    barrier = pltpu.get_barrier_semaphore()
+    for axis in AXES:
+        for by in (1, -1):
+            pl.semaphore_signal(barrier, inc=1, device_id=device_of(shifted(pos, axis, by)), device_id_type=MESH)
+    n_layers = own_k.shape[0]
+    placed = []
+    for src, dst in ((own_k, all_k), (own_v, all_v)):
+        for layer in range(n_layers):
+            mine = dst.at[layer, pos["z"], pos["y"], pos["x"]]
+            put = pltpu.make_async_copy(src.at[layer], mine, local_sem.at[len(placed)])
+            put.start()
+            placed.append(put)
+    pl.semaphore_wait(barrier, 6)
+    for put in placed:
+        put.wait()
+    whole = [dst.at[layer] for layer in range(n_layers) for dst in (all_k, all_v)]
+    jobs = [(t, color) for t in range(len(whole)) for color in range(3)]
+    sent = []
+    ready = {}
+    for stage in range(3):
+        copies = {
+            (t, color): ring_copies(whole[t], color, stage, pos, send_sem.at[t, color, stage], recv_sem.at[t, color, stage])
+            for t, color in jobs
+        }
+        for job in jobs:
+            for done in ready.get(job, ()):
+                done.wait_recv()
+            for first in copies[job][:2]:
+                first.start()
+        for job in jobs:
+            copies[job][0].wait_recv()
+            copies[job][2].start()
+            copies[job][1].wait_recv()
+            copies[job][3].start()
+            ready[job] = copies[job][2:]
+            sent.extend(copies[job])
+    for job in jobs:
+        for done in ready[job]:
+            done.wait_recv()
+    for one in sent:
+        one.wait_send()
+
+
+def gather_patches(own_k, own_v):
+    n_layers, rows, width = own_k.shape
+    full = jax.ShapeDtypeStruct((n_layers, RING, RING, RING, rows, width), own_k.dtype)
+    out_k, out_v = pl.pallas_call(
+        gather_kernel,
+        out_shape=(full, full),
+        in_specs=[pl.BlockSpec(memory_space=pltpu.VMEM)] * 2,
+        out_specs=[pl.BlockSpec(memory_space=pl.ANY)] * 2,
+        scratch_shapes=[
+            pltpu.SemaphoreType.DMA((2 * n_layers,)),
+            pltpu.SemaphoreType.DMA((2 * n_layers, 3, 3, 4)),
+            pltpu.SemaphoreType.DMA((2 * n_layers, 3, 3, 4)),
+        ],
+        compiler_params=pltpu.CompilerParams(collective_id=0, has_side_effects=True),
+        name="torus_gather",
+    )(own_k, own_v)
+    tokens = RING * RING * RING * rows
+    return out_k.reshape(n_layers, tokens, width), out_v.reshape(n_layers, tokens, width)
+
+
 def solution(mesh):
     n_cfg = mesh.shape["cfg"]
     partner = [(dev_pos, dev_pos ^ 1) for dev_pos in range(n_cfg)]
@@ -43,6 +172,7 @@
         local_rows = latent.shape[1]
         n_heads = w_out.shape[1]
         head_dim = w_out.shape[2]
+        n_steps = sched_coef.shape[1]
         cfg_slot = lax.axis_index("cfg")
         row_start = lax.axis_index("patch") * local_rows
         is_cond = cfg_slot % 2 == 0
@@ -50,7 +180,7 @@
         mod_all = jnp.einsum("td,lde->tle", jax.nn.silu(cond_vec[0]).astype(jnp.bfloat16), w_ada, preferred_element_type=jnp.float32)
         k_cache = [k_stale[0, layer_idx] for layer_idx in range(n_layers)]
         v_cache = [v_stale[0, layer_idx] for layer_idx in range(n_layers)]
-        for step_idx in range(sched_coef.shape[1]):
+        for step_idx in range(n_steps):
             resid_now = latent_now
             k_next = []
             v_next = []
@@ -59,8 +189,12 @@
                 norm_attn = (layer_norm(resid_now) * (1.0 + scale_attn) + shift_attn).astype(jnp.bfloat16)
                 qkv_all = jnp.dot(norm_attn, w_qkv[layer_idx], preferred_element_type=jnp.float32).astype(jnp.bfloat16)
                 q_new, k_new, v_new = jnp.split(qkv_all, 3, axis=-1)
-                k_next.append(lax.all_gather(k_new, "patch", axis=0, tiled=True))
-                v_next.append(lax.all_gather(v_new, "patch", axis=0, tiled=True))
+                if step_idx < n_steps - 1:
+                    k_next.append(lax.all_gather(k_new, "patch", axis=0, tiled=True))
+                    v_next.append(lax.all_gather(v_new, "patch", axis=0, tiled=True))
+                else:
+                    k_next.append(k_new)
+                    v_next.append(v_new)
                 key_set = lax.dynamic_update_slice(k_cache[layer_idx], k_new, (row_start, 0))
                 value_set = lax.dynamic_update_slice(v_cache[layer_idx], v_new, (row_start, 0))
                 heads_out = attend(q_new, key_set, value_set, n_heads, head_dim)
@@ -79,7 +213,8 @@
             eps_unc = jnp.where(is_cond, eps_peer, eps_own).astype(jnp.float32)
             guided = eps_unc + sched_coef[2, step_idx] * (eps_cond - eps_unc)
             latent_now = sched_coef[0, step_idx] * latent_now + sched_coef[1, step_idx] * guided
-        return latent_now[None], jnp.stack(k_cache)[None], jnp.stack(v_cache)[None]
+        k_last, v_last = gather_patches(jnp.stack(k_cache), jnp.stack(v_cache))
+        return latent_now[None], k_last[None], v_last[None]
 
     return jax.shard_map(
         local_step,

time: 914 us -> 854 us (0.934)
  waiting for transfers between devices: 243 us -> 2.43 us
  Pallas kernels: 0 us -> 188 us
  other arithmetic: 54.2 us -> 15 us
  local copies, waits for them, and re-layouts: 116 us -> 149 us
    pallas_call x0 -> x1, Pallas kernels: none -> 188 us  [gather_patches(): pl.pallas_call(gather_kernel, out_shape=(full, full), in_specs=[pl.BlockS...]
    all_gather x4 -> x2, waiting for transfers between devices: 166 us -> 0.69 us  [local_step(): v_next.append(lax.all_gather(v_new, 'patch', axis=0, tiled=True))]
    all_gather x4 -> x2, waiting for transfers between devices: 72.3 us -> 0.04 us  [local_step(): k_next.append(lax.all_gather(k_new, 'patch', axis=0, tiled=True))]
    broadcast_in_dim x3 -> x1, other arithmetic: 43.8 us -> 3.02 us  [local_step(): return (latent_now[None], k_last[None], v_last[None])]
    unnamed x42 -> x60, local copies, waits for them, and re-layouts: 10.9 us -> 44 us
  transfers between devices with their start and end apart: 10 -> 6, of which waited for: 6 -> 2; matrix products, arithmetic and copies ran while one was open for 54% -> 43% of each run, Pallas kernels for 0% -> 22%
where the time goes in v1:
time: 854 us; the launch traced here: 847 us
  matrix products  476 us (56%)
  Pallas kernels  188 us (22%)
  local copies, waits for them, and re-layouts  149 us (17%)
  other arithmetic  15 us (2%)
  between operations  14.4 us (2%)
    pallas_call x1, Pallas kernels, gather_patches(): pl.pallas_call(gather_kernel, out_shape=(full, full), in_specs=[pl.BlockS...  188 us
    dot_general x4, matrix products, local_step(): jnp.dot(norm_mlp, w_up[layer_idx], preferred_element_type=jnp.float32)  107 us
    dot_general x4, matrix products, local_step(): jnp.dot(mlp_act, w_down[layer_idx], preferred_element_type=jnp.float32)  106 us
    dot_general x4, matrix products, local_step(): jnp.dot(norm_attn, w_qkv[layer_idx], preferred_element_type=jnp.float32)  83.6 us
    dot_general x1, matrix products, local_step(): jnp.einsum('td,lde->tle', jax.nn.silu(cond_vec[0]).astype(jnp.bfloat16),...  69.9 us
    reshape x4, local copies, waits for them, and re-layouts, attend(): val_h = value_set.reshape(tokens, n_heads, head_dim)  66.4 us
    dot_general x4, matrix products, local_step(): jnp.einsum('qhe,hed->qd', heads_out, w_out[layer_idx], preferred_element_...  60 us
    unnamed x60, local copies, waits for them, and re-layouts  44 us
  transfers between devices with their start and end apart: 6, of which 2 were waited for; matrix products, arithmetic and copies ran while one was open for 43% of the time, Pallas kernels for 22%

profile of v1, /device:TPU:1, one launch (start us, length us, event | category | flops | bytes accessed | tf_op | source)
XLA Modules:
  0.0 847.0 jit_solution(5728081258344852517)
XLA Ops:
  7.2 69.9 %fusion.356 = f32[2,2,18432]{2,0,1:T(2,128)S(1)} fusion(bf16[2,3072,18432]{2,1,0:T(8,128)(2,1)} %param.14, f32[1,2,3072]{2,1,0:T(2,128)} %param.12), kind=kOutput, calls=%fused_computation.298 | convolution fusion | flops 453015552 | bytes 226811904 | tf_op jit(solution)/shard_map/td,lde->tle/dot_general | solution.py:180
  77.6 33.9 %slice_bitcast_fusion = (bf16[2048,3072]{1,0:T(8,128)(2,1)}, bf16[2048,3072]{1,0:T(8,128)(2,1)}, bf16[2048,3072]{1,0:T(8,128)(2,1)}, bf16[2048,3072]{1,0:T(8,128)(2,1)}) fusion(bf16[1,2,2048,3072]{3,2,1,0:T(8,128)(2,1)} %param.20, bf16[1,2,2048,3072]{3,2,1,0:T(8,128)(2,1)} %param.21), kind=kLoop, calls=%fused_computation.60 | loop fusion | bytes 100663296 | tf_op jit(solution)/shard_map/squeeze | solution.py:181
  111.5 20.9 %fusion.60 = bf16[32,9216]{1,0:T(8,128)(2,1)S(1)} fusion(bf16[2,3072,9216]{2,1,0:T(8,128)(2,1)} %param.15, bf16[1,32,3072]{2,1,0:T(8,128)(2,1)S(1)} %copy-done.6, f32[3072]{0:T(1024)S(1)} %bitcast.422, f32[3072]{0:T(1024)S(1)} %bitcast.423, f32[32]{0:T(128)S(1)} %add_rsqrt_fusion.9, f32[32]{0:T(128)S(1)} %broadcast_multiply_fusion.9), kind=kOutput, calls=%fused_computation.64 | convolution fusion | flops 1812824064 | bytes 57434368 | tf_op jit(solution)/shard_map/dot_general | solution.py:190
  134.2 16.6 %copy.26 = bf16[2048,3072]{0,1:T(8,128)(2,1)} copy(bf16[2048,3072]{1,0:T(8,128)(2,1)} %get-tuple-element.89) | data formatting | bytes 25165824 | tf_op jit(solution)/shard_map/reshape | solution.py:27
  162.2 15.0 %fusion.391 = (f32[32]{0:T(128)S(1)}, f32[32,3072]{1,0:T(8,128)S(1)}) fusion(bf16[2,24,128,3072]{3,2,1,0:T(8,128)(2,1)} %param.16, bf16[2048,24,128]{0,2,1:T(8,128)(2,1)} %bitcast.394, f32[24,32,2048]{2,1,0:T(8,128)} %copy-done.2, f32[24,32]{1,0:T(8,128)S(1)} %get-tuple-element.123, f32[32,24]{0,1:T(8,128)S(1)} %bitcast.399, f32[3072]{0:T(1024)S(1)} %bitcast.419, ...), kind=kOutput, calls=%fused_computation.351 | convolution fusion | flops 1011941376 | bytes 38357120 | tf_op jit(solution)/shard_map/qhe,hed->qd/dot_general | solution.py:201
  178.3 26.8 %fusion.165.clone.1.clone.5 = bf16[32,12288]{1,0:T(8,128)(2,1)S(1)} fusion(bf16[2,3072,12288]{2,1,0:T(8,128)(2,1)} %param.17, f32[32,3072]{1,0:T(8,128)S(1)} %get-tuple-element.126, f32[3072]{0:T(1024)S(1)} %bitcast.424, f32[3072]{0:T(1024)S(1)} %bitcast.414, f32[32]{0:T(128)S(1)} %add_rsqrt_fusion.8, ...), kind=kOutput, calls=%fused_computation.129.clone.clone.clone.clone.clone.2 | convolution fusion | flops 2419949568 | bytes 76701952 | tf_op jit(solution)/shard_map/dot_general | solution.py:204
  205.1 26.3 %fusion.394 = (f32[32]{0:T(128)S(1)}, f32[32,3072]{1,0:T(8,128)S(1)}) fusion(f32[32,3072]{1,0:T(8,128)S(1)} %get-tuple-element.126, bf16[2,12288,3072]{2,1,0:T(8,128)(2,1)} %param.18, f32[3072]{0:T(1024)S(1)} %bitcast.413, bf16[32,12288]{1,0:T(8,128)(2,1)S(1)} %fusion.165.clone.1.clone.5), kind=kOutput, calls=%fused_computation.352 | convolution fusion | flops 2416214016 | bytes 77082752 | tf_op jit(solution)/shard_map/dot_general | solution.py:206
  231.6 21.2 %fusion.66 = bf16[32,9216]{1,0:T(8,128)(2,1)S(1)} fusion(bf16[2,3072,9216]{2,1,0:T(8,128)(2,1)} %param.15, f32[32,3072]{1,0:T(8,128)S(1)} %get-tuple-element.128, f32[3072]{0:T(1024)S(1)} %bitcast.420, f32[3072]{0:T(1024)S(1)} %bitcast.421, f32[32]{0:T(128)S(1)} %add_rsqrt_fusion.7, f32[32]{0:T(128)S(1)} %broadcast_multiply_fusion.7), kind=kOutput, calls=%fused_computation.66 | convolution fusion | flops 1812725760 | bytes 57630976 | tf_op jit(solution)/shard_map/dot_general | solution.py:190
  254.3 16.6 %copy.27 = bf16[2048,3072]{0,1:T(8,128)(2,1)} copy(bf16[2048,3072]{1,0:T(8,128)(2,1)} %get-tuple-element.84) | data formatting | bytes 25165824 | tf_op jit(solution)/shard_map/reshape | solution.py:27
  282.3 15.0 %fusion.397 = (f32[32]{0:T(128)S(1)}, f32[32,3072]{1,0:T(8,128)S(1)}) fusion(f32[32,3072]{1,0:T(8,128)S(1)} %get-tuple-element.128, bf16[2,24,128,3072]{3,2,1,0:T(8,128)(2,1)} %param.16, bf16[2048,24,128]{0,2,1:T(8,128)(2,1)} %bitcast.393, f32[24,32,2048]{2,1,0:T(8,128)} %copy-done, f32[24,32]{1,0:T(8,128)S(1)} %get-tuple-element.129, ...), kind=kOutput, calls=%fused_computation.353 | convolution fusion | flops 1011843072 | bytes 38553728 | tf_op jit(solution)/shard_map/qhe,hed->qd/dot_general | solution.py:201
  297.5 26.8 %fusion.179.clone.1.clone.5 = bf16[32,12288]{1,0:T(8,128)(2,1)S(1)} fusion(bf16[2,3072,12288]{2,1,0:T(8,128)(2,1)} %param.17, f32[32,3072]{1,0:T(8,128)S(1)} %get-tuple-element.132, f32[3072]{0:T(1024)S(1)} %bitcast.416, f32[3072]{0:T(1024)S(1)} %bitcast.417, f32[32]{0:T(128)S(1)} %add_rsqrt_fusion.6, ...), kind=kOutput, calls=%fused_computation.137.clone.clone.clone.clone.clone.2 | convolution fusion | flops 2419949568 | bytes 76701952 | tf_op jit(solution)/shard_map/dot_general | solution.py:204
  324.3 26.5 %fusion.400 = (f32[32]{0:T(128)S(1)}, f32[32,3072]{1,0:T(8,128)S(1)}) fusion(f32[32,3072]{1,0:T(8,128)S(1)} %get-tuple-element.132, bf16[2,12288,3072]{2,1,0:T(8,128)(2,1)} %param.18, f32[3072]{0:T(1024)S(1)} %bitcast.415, bf16[32,12288]{1,0:T(8,128)(2,1)S(1)} %fusion.179.clone.1.clone.5), kind=kOutput, calls=%fused_computation.354 | convolution fusion | flops 2416214016 | bytes 77082752 | tf_op jit(solution)/shard_map/dot_general | solution.py:206
  365.9 20.8 %fusion.63 = bf16[32,9216]{1,0:T(8,128)(2,1)S(1)} fusion(bf16[2,3072,9216]{2,1,0:T(8,128)(2,1)} %param.15, f32[32,3072]{1,0:T(8,128)S(1)} %get-tuple-element.53, f32[3072]{0:T(1024)S(1)} %bitcast.411, f32[3072]{0:T(1024)S(1)} %bitcast.412, f32[32]{0:T(128)S(1)} %add_rsqrt_fusion.4, f32[32]{0:T(128)S(1)} %broadcast_multiply_fusion.4), kind=kOutput, calls=%fused_computation.65 | convolution fusion | flops 1812725760 | bytes 57630976 | tf_op jit(solution)/shard_map/dot_general | solution.py:190
  387.7 16.6 %copy.28 = bf16[2048,3072]{0,1:T(8,128)(2,1)} copy(bf16[2048,3072]{1,0:T(8,128)(2,1)} %get-tuple-element.72) | data formatting | bytes 25165824 | tf_op jit(solution)/shard_map/reshape | solution.py:27
  415.7 15.0 %fusion.403 = (f32[32]{0:T(128)S(1)}, f32[32,3072]{1,0:T(8,128)S(1)}) fusion(f32[32,3072]{1,0:T(8,128)S(1)} %get-tuple-element.53, bf16[2,24,128,3072]{3,2,1,0:T(8,128)(2,1)} %param.16, bf16[2048,24,128]{0,2,1:T(8,128)(2,1)} %bitcast.396, f32[24,32,2048]{2,1,0:T(8,128)} %copy-done.3, f32[24,32]{1,0:T(8,128)S(1)} %get-tuple-element.135, ...), kind=kOutput, calls=%fused_computation.355 | convolution fusion | flops 1011843072 | bytes 38553728 | tf_op jit(solution)/shard_map/qhe,hed->qd/dot_general | solution.py:201
  430.9 26.8 %fusion.193.clone.1.clone.2 = bf16[32,12288]{1,0:T(8,128)(2,1)S(1)} fusion(bf16[2,3072,12288]{2,1,0:T(8,128)(2,1)} %param.17, f32[32,3072]{1,0:T(8,128)S(1)} %get-tuple-element.138, f32[3072]{0:T(1024)S(1)} %bitcast.408, f32[3072]{0:T(1024)S(1)} %bitcast.409, f32[32]{0:T(128)S(1)} %add_rsqrt_fusion.3, ...), kind=kOutput, calls=%fused_computation.145.clone.clone.clone.clone.clone | convolution fusion | flops 2419949568 | bytes 76701952 | tf_op jit(solution)/shard_map/dot_general | solution.py:204
  457.8 26.7 %fusion.406 = (f32[32]{0:T(128)S(1)}, f32[32,3072]{1,0:T(8,128)S(1)}) fusion(f32[32,3072]{1,0:T(8,128)S(1)} %get-tuple-element.138, bf16[2,12288,3072]{2,1,0:T(8,128)(2,1)} %param.18, f32[3072]{0:T(1024)S(1)} %bitcast.407, bf16[32,12288]{1,0:T(8,128)(2,1)S(1)} %fusion.193.clone.1.clone.2), kind=kOutput, calls=%fused_computation.356 | convolution fusion | flops 2416214016 | bytes 77082752 | tf_op jit(solution)/shard_map/dot_general | solution.py:206
  484.7 20.8 %fusion.69 = bf16[32,9216]{1,0:T(8,128)(2,1)S(1)} fusion(bf16[2,3072,9216]{2,1,0:T(8,128)(2,1)} %param.15, f32[32,3072]{1,0:T(8,128)S(1)} %get-tuple-element.140, f32[3072]{0:T(1024)S(1)} %bitcast.405, f32[3072]{0:T(1024)S(1)} %bitcast.406, f32[32]{0:T(128)S(1)} %add_rsqrt_fusion.2, f32[32]{0:T(128)S(1)} %broadcast_multiply_fusion.2), kind=kOutput, calls=%fused_computation.67 | convolution fusion | flops 1812725760 | bytes 57630976 | tf_op jit(solution)/shard_map/dot_general | solution.py:190
  507.1 16.6 %copy.29 = bf16[2048,3072]{0,1:T(8,128)(2,1)} copy(bf16[2048,3072]{1,0:T(8,128)(2,1)} %get-tuple-element.82) | data formatting | bytes 25165824 | tf_op jit(solution)/shard_map/reshape | solution.py:27
  535.0 15.0 %fusion.409 = (f32[32]{0:T(128)S(1)}, f32[32,3072]{1,0:T(8,128)S(1)}) fusion(f32[32,3072]{1,0:T(8,128)S(1)} %get-tuple-element.140, bf16[2,24,128,3072]{3,2,1,0:T(8,128)(2,1)} %param.16, bf16[2048,24,128]{0,2,1:T(8,128)(2,1)} %bitcast.395, f32[24,32,2048]{2,1,0:T(8,128)} %copy-done.1, f32[24,32]{1,0:T(8,128)S(1)} %get-tuple-element.141, ...), kind=kOutput, calls=%fused_computation.357 | convolution fusion | flops 1011843072 | bytes 38553728 | tf_op jit(solution)/shard_map/qhe,hed->qd/dot_general | solution.py:201
  550.3 27.0 %fusion.207.clone.1.clone.2 = bf16[32,12288]{1,0:T(8,128)(2,1)S(1)} fusion(bf16[2,3072,12288]{2,1,0:T(8,128)(2,1)} %param.17, f32[32,3072]{1,0:T(8,128)S(1)} %get-tuple-element.144, f32[3072]{0:T(1024)S(1)} %bitcast.402, f32[3072]{0:T(1024)S(1)} %bitcast.403, f32[32]{0:T(128)S(1)} %add_rsqrt_fusion.1, ...), kind=kOutput, calls=%fused_computation.153.clone.clone.clone.clone.clone | convolution fusion | flops 2419949568 | bytes 76701952 | tf_op jit(solution)/shard_map/dot_general | solution.py:204
  577.3 26.3 %fusion.412 = (f32[32]{0:T(128)S(1)}, f32[32,3072]{1,0:T(8,128)S(1)}) fusion(f32[32,3072]{1,0:T(8,128)S(1)} %get-tuple-element.144, bf16[2,12288,3072]{2,1,0:T(8,128)(2,1)} %param.18, f32[3072]{0:T(1024)S(1)} %bitcast.401, bf16[32,12288]{1,0:T(8,128)(2,1)S(1)} %fusion.207.clone.1.clone.2), kind=kOutput, calls=%fused_computation.358 | convolution fusion | flops 2416214016 | bytes 77082752 | tf_op jit(solution)/shard_map/dot_general | solution.py:206
  616.3 187.9 %torus_gather.1 = (bf16[2,4,4,4,32,3072]{5,4,3,2,1,0:T(8,128)(2,1)}, bf16[2,4,4,4,32,3072]{5,4,3,2,1,0:T(8,128)(2,1)}) custom-call(bf16[2,32,3072]{2,1,0:T(8,128)(2,1)} %pad_maximum_fusion.own_k, bf16[2,32,3072]{2,1,0:T(8,128)(2,1)} %pad_maximum_fusion.1.own_v), custom_call_target="tpu_custom_call" | custom-call | tf_op jit(solution)/shard_map/torus_gather/pallas_call | solution.py:146
  807.2 24.1 %copy.96 = bf16[1,2,2048,3072]{3,2,1,0:T(8,128)(2,1)} copy(bf16[1,2,2048,3072]{3,2,1,0:T(8,128)(2,1)} %bitcast.392) | data formatting | bytes 50331648
  (128 shorter events, 93.8 us)
Async XLA Ops:
  7.2 379.5 %all-gather.7.cloned.1.call-start = ((), (), s32[]{:S(2)}) async-start(), calls=%async_computation.1 | async-start | bytes 12779520 | tf_op jit(solution)/shard_map/all_gather | solution.py:193
  7.2 69.9 %copy-start.6 = (bf16[1,32,3072]{2,1,0:T(8,128)(2,1)S(1)}, bf16[1,32,3072]{2,1,0:T(8,128)(2,1)}, u32[]{:S(2)}) copy-start(bf16[1,32,3072]{2,1,0:T(8,128)(2,1)} %param.11) | copy-start | bytes 589828
  133.3 253.5 %all-gather.5.cloned.1.call-start = ((), (), s32[]{:S(2)}) async-start(), calls=%async_computation | async-start | bytes 12779520 | tf_op jit(solution)/shard_map/all_gather | solution.py:194
  134.0 371.5 %all-gather.11.cloned.1.call-start = ((), (), s32[]{:S(2)}) async-start(), calls=%async_computation.3 | async-start | bytes 12779520 | tf_op jit(solution)/shard_map/all_gather | solution.py:193
  253.8 252.4 %all-gather.9.cloned.1.call-start = ((), (), s32[]{:S(2)}) async-start(), calls=%async_computation.2 | async-start | bytes 12779520 | tf_op jit(solution)/shard_map/all_gather | solution.py:194
  351.1 14.8 %copy-start.20 = (f32[1,1,3072]{2,0,1:T(1,128)S(1)}, f32[1,1,3072]{2,0,1:T(1,128)}, u32[]{:S(2)}) copy-start(f32[1,1,3072]{2,0,1:T(1,128)} %get-tuple-element.102) | copy-start | bytes 36868
  360.9 2.5 collective-permute-start
  365.6 50.0 %copy-start.4 = (f32[32,3072]{1,0:T(8,128)}, f32[32,3072]{1,0:T(8,128)S(1)}, u32[]{:S(2)}) copy-start(f32[32,3072]{1,0:T(8,128)S(1)} %get-tuple-element.53) | copy-start | bytes 1179652
  415.7 15.3 %copy-start.17 = (f32[1,1,3072]{2,0,1:T(1,128)S(1)}, f32[1,1,3072]{2,0,1:T(1,128)}, u32[]{:S(2)}) copy-start(f32[1,1,3072]{2,0,1:T(1,128)} %get-tuple-element.99) | copy-start | bytes 36868
  415.7 15.3 %copy-start.18 = (f32[1,1,3072]{2,0,1:T(1,128)S(1)}, f32[1,1,3072]{2,0,1:T(1,128)}, u32[]{:S(2)}) copy-start(f32[1,1,3072]{2,0,1:T(1,128)} %get-tuple-element.100) | copy-start | bytes 36868
  430.9 26.8 %copy-start.16 = (f32[1,1,3072]{2,0,1:T(1,128)S(1)}, f32[1,1,3072]{2,0,1:T(1,128)}, u32[]{:S(2)}) copy-start(f32[1,1,3072]{2,0,1:T(1,128)} %get-tuple-element.101) | copy-start | bytes 36868
  457.8 26.9 %copy-start.14 = (f32[1,1,3072]{2,0,1:T(1,128)S(1)}, f32[1,1,3072]{2,0,1:T(1,128)}, u32[]{:S(2)}) copy-start(f32[1,1,3072]{2,0,1:T(1,128)} %get-tuple-element.96) | copy-start | bytes 36868
  457.8 26.9 %copy-start.15 = (f32[1,1,3072]{2,0,1:T(1,128)S(1)}, f32[1,1,3072]{2,0,1:T(1,128)}, u32[]{:S(2)}) copy-start(f32[1,1,3072]{2,0,1:T(1,128)} %get-tuple-element.97) | copy-start | bytes 36868
  535.0 15.3 %copy-start.11 = (f32[1,1,3072]{2,0,1:T(1,128)S(1)}, f32[1,1,3072]{2,0,1:T(1,128)}, u32[]{:S(2)}) copy-start(f32[1,1,3072]{2,0,1:T(1,128)} %get-tuple-element.94) | copy-start | bytes 36868
  535.0 15.3 %copy-start.12 = (f32[1,1,3072]{2,0,1:T(1,128)S(1)}, f32[1,1,3072]{2,0,1:T(1,128)}, u32[]{:S(2)}) copy-start(f32[1,1,3072]{2,0,1:T(1,128)} %get-tuple-element.95) | copy-start | bytes 36868
  550.3 27.0 %copy-start.10 = (f32[1,1,3072]{2,0,1:T(1,128)S(1)}, f32[1,1,3072]{2,0,1:T(1,128)}, u32[]{:S(2)}) copy-start(f32[1,1,3072]{2,0,1:T(1,128)} %get-tuple-element.93) | copy-start | bytes 36868
  603.9 200.3 %copy-start.5 = (f32[32,3072]{1,0:T(8,128)S(1)}, f32[32,3072]{1,0:T(8,128)}, u32[]{:S(2)}) copy-start(f32[32,3072]{1,0:T(8,128)} %copy-done.4) | copy-start | bytes 1179652
  613.7 190.4 %collective-permute-start.1 = (bf16[32,3072]{1,0:T(8,128)(2,1)S(1)}, bf16[32,3072]{1,0:T(8,128)(2,1)S(1)}, u32[]{:S(2)}, u32[]{:S(2)}) collective-permute-start(bf16[32,3072]{1,0:T(8,128)(2,1)S(1)} %convolution_convert_fusion), channel_id=1, source_target_pairs={{0,64},{64,0},{1,65},{65,1},{2,66},{66,2},{3,67},{67,3},{4,68},{68... | collective-permute-start | bytes 589832 | tf_op jit(solution)/shard_map/ppermute | solution.py:211
  804.2 27.1 %slice-start = ((s8[25165824]{0:T(1024)(128)(4,1)}), s8[4194304]{0:T(1024)(128)(4,1)S(1)}, s32[]{:S(2)}) async-start(s8[25165824]{0:T(1024)(128)(4,1)} %bitcast.389), calls=%async_computation.4 | async-start | bytes 8388608
  807.2 24.1 %slice-start.1 = ((s8[25165824]{0:T(1024)(128)(4,1)}), s8[4194304]{0:T(1024)(128)(4,1)S(1)}, s32[]{:S(2)}) async-start(s8[25165824]{0:T(1024)(128)(4,1)} %bitcast.389), calls=%async_computation.5 | async-start | bytes 8388608
  807.2 24.1 %slice-start.2 = ((s8[25165824]{0:T(1024)(128)(4,1)}), s8[4194304]{0:T(1024)(128)(4,1)S(1)}, s32[]{:S(2)}) async-start(s8[25165824]{0:T(1024)(128)(4,1)} %bitcast.389), calls=%async_computation.6 | async-start | bytes 8388608
  807.2 24.1 %slice-start.3 = ((s8[25165824]{0:T(1024)(128)(4,1)}), s8[4194304]{0:T(1024)(128)(4,1)S(1)}, s32[]{:S(2)}) async-start(s8[25165824]{0:T(1024)(128)(4,1)} %bitcast.389), calls=%async_computation.7 | async-start | bytes 8388608
  807.2 24.1 %slice-start.4 = ((s8[25165824]{0:T(1024)(128)(4,1)}), s8[4194304]{0:T(1024)(128)(4,1)S(1)}, s32[]{:S(2)}) async-start(s8[25165824]{0:T(1024)(128)(4,1)} %bitcast.389), calls=%async_computation.8 | async-start | bytes 8388608
  807.2 24.1 %slice-start.5 = ((s8[25165824]{0:T(1024)(128)(4,1)}), s8[4194304]{0:T(1024)(128)(4,1)S(1)}, s32[]{:S(2)}) async-start(s8[25165824]{0:T(1024)(128)(4,1)} %bitcast.389), calls=%async_computation.9 | async-start | bytes 8388608
  (11 other events, 94.5 us)
Sparse Core Ops, SparseCore 0:
  133.4 93.6 all-gather.6
  229.8 90.2 all-gather.4
  322.9 90.2 all-gather.10
  415.8 90.3 all-gather.8

commit v2 on v0

v2 whole, which is shorter than its diff:
```python
import functools

import jax
import jax.numpy as jnp
from jax import lax
from jax.experimental import pallas as pl
from jax.experimental.pallas import tpu as pltpu
from jax.sharding import PartitionSpec as P

RING = 4
AXES = ("z", "y", "x")
COLOR_ORDERS = (("x", "y", "z"), ("y", "z", "x"), ("z", "x", "y"))
SHARE_ORDERS = (("y", "x"), ("x", "y"))
MESH = pl.DeviceIdType.MESH
F32 = jnp.float32
BF16 = jnp.bfloat16
HEAD = 128
TILE = 512
SUB = 256
WIDE = 2 * TILE
BUFFERS = 11
STEPS = 2
LAYERS = 2
K, V, Q = 0, 1, 2


def dot(lhs, rhs):
    return jnp.dot(lhs, rhs, preferred_element_type=F32)


def torus_position():
    patch = lax.axis_index("patch")
    return {"z": lax.div(patch, RING * RING), "y": lax.rem(lax.div(patch, RING), RING), "x": lax.rem(patch, RING)}


def patch_at(pos):
    return (pos["z"] * RING + pos["y"]) * RING + pos["x"]


class Torus:
    def __init__(self):
        self.pos = torus_position()
        self.coord, self.patch = {}, {}
        for axis in AXES:
            for by in range(1, RING):
                coord = lax.rem(self.pos[axis] + by, RING)
                self.coord[axis, by] = coord
                self.patch[axis, by] = patch_at({**self.pos, axis: coord})


def remote(src, dst, send_sem, recv_sem, **device_id):
    return pltpu.make_async_remote_copy(
        src_ref=src, dst_ref=dst, send_sem=send_sem, recv_sem=recv_sem, device_id=device_id, device_id_type=MESH
    )


class Ring:
    def __init__(self, torus, axis, view, send_sem, recv_sem):
        me, succ, prev = torus.pos[axis], torus.coord[axis, 1], torus.coord[axis, RING - 1]
        ahead, behind = torus.patch[axis, 1], torus.patch[axis, RING - 1]
        self.sends = ((me, None, ahead), (me, None, behind), (prev, 0, ahead), (succ, 1, behind))
        self.parts = (view, send_sem, recv_sem)

    def copy(self, slot):
        view, send_sem, recv_sem = self.parts
        coord, half, patch = self.sends[slot]
        part = view(coord, half)
        return remote(part, part, send_sem(slot), recv_sem(slot), patch=patch)

    def first(self):
        for slot in (0, 1):
            self.copy(slot).start()

    def relay(self):
        for slot in (0, 1):
            self.copy(slot).wait_recv()
            self.copy(slot + 2).start()

    def settle(self):
        for slot in (2, 3):
            self.copy(slot).wait_recv()

    def drain(self):
        for slot in range(4):
            self.copy(slot).wait_send()


def full_rings(ref, color, torus, send_sem, recv_sem):
    width = ref.shape[4]
    cut = [0, width // 3 // SUB * SUB, width // 3 // SUB * SUB * 2, width]
    base, size = cut[color], cut[color + 1] - cut[color]
    order = COLOR_ORDERS[color]

    def stage(k):
        axis = order[k]

        def view(coord, half):
            index = []
            for name in AXES:
                index.append(coord if name == axis else slice(None) if name in order[:k] else torus.pos[name])
            columns = pl.ds(base, size) if half is None else pl.ds(base + half * (size // 2), size // 2)
            return ref.at[(*index, slice(None), columns)]

        return Ring(torus, axis, view, lambda slot: send_sem.at[k, slot], lambda slot: recv_sem.at[k, slot])

    return [stage(k) for k in range(3)]


def share_rings(ref, color, torus, send_sem, recv_sem):
    size = ref.shape[4] // 2
    order = SHARE_ORDERS[color]
    columns = pl.ds(color * size, size)

    def stage(k):
        axis = order[k]

        def view(coord, half):
            planes = slice(None) if half is None else pl.ds(half * (RING // 2), RING // 2)
            index = [coord if name == axis else slice(None) if name in order[:k] else torus.pos[name] for name in ("y", "x")]
            return ref.at[(planes, *index, slice(None), columns)]

        return Ring(torus, axis, view, lambda slot: send_sem.at[k, slot], lambda slot: recv_sem.at[k, slot])

    return [stage(k) for k in range(2)]


def denoise_kernel(
    lat, cond, sched, w_ada, w_qkv, w_out, w_up, w_down, w_head, k_old, v_old,
    lat_out, all_k, all_v, shared,
    wbuf, kbuf, vbuf, xs, r, h, act, out_own, out_peer, down_own, down_peer, sb, rb, o_own, ob, mod, cond_peer, scores,
    w_sem, kv_sem, cond_sem, mod_send, mod_recv, qkv_send, qkv_recv, o_send, o_recv, out_send, out_recv, down_send, down_recv,
    x_sem, share_put, share_send, share_recv, own_put, own_send, own_recv, full_send, full_recv,
):
    rows, width = lat.shape
    half = width // 2
    group = width // RING
    chunk = width // 8
    hidden = w_up.shape[2] // 2
    n_qkv = half // TILE
    n_out = width // WIDE
    n_up = hidden // TILE
    n_deep = hidden // half
    n_down = n_out * n_deep
    n_head = half // TILE
    n_block = 3 * n_qkv + n_out + n_up + n_down
    n_step = LAYERS * n_block + n_head
    n_ada = 3
    n_tiles = n_ada + STEPS * n_step
    n_buf = wbuf.shape[0]
    scale = HEAD**-0.5

    c = lax.axis_index("cfg")
    other = 1 - c
    torus = Torus()
    z, y, x = (torus.pos[axis] for axis in AXES)
    z_core = lax.div(z, 2)
    z_odd = lax.rem(z, 2)
    z_patch = [(v * RING + y) * RING + x for v in range(RING)]
    pair_patch = [((2 * c + g) * RING + y) * RING + x for g in range(2)]

    def put(src, dst, slot):
        pltpu.make_async_copy(src, dst, w_sem.at[slot]).start()

    def put_deep(ref, col, slot):
        col = pl.multiple_of(col, TILE)
        for k in range(2):
            put(ref.at[pl.ds(k * half, half), pl.ds(col, TILE)], wbuf.at[slot, :, pl.ds(k * TILE, TILE)], slot)

    def put_wide(ref, row, col, slot):
        row = pl.multiple_of(row, half)
        col = pl.multiple_of(col, WIDE)
        put(ref.at[pl.ds(row, half), pl.ds(col, WIDE)], wbuf.at[slot], slot)

    def issue_ada(i):
        col = pl.multiple_of(((y * RING + x) * n_ada + i) * chunk, chunk)
        for k in range(2):
            put(w_ada.at[c, pl.ds(k * half, half), pl.ds(col, chunk)], wbuf.at[i, :, pl.ds(k * chunk, chunk)], i)

    def issue(n):
        slot = lax.rem(n, n_buf)
        inside = lax.rem(n - n_ada, n_step)
        layer = lax.div(inside, n_block)
        u = lax.rem(inside, n_block)
        live = n < n_tiles
        block = live & (inside < LAYERS * n_block)
        at_out, at_up, at_down = 3 * n_qkv, 3 * n_qkv + n_out, 3 * n_qkv + n_out + n_up

        @pl.when(block & (u < at_out))
        def _():
            part = lax.rem(lax.div(u, n_qkv) + 1, 3)
            put_deep(w_qkv.at[layer], part * width + c * half + lax.rem(u, n_qkv) * TILE, slot)

        @pl.when(block & (u >= at_out) & (u < at_up))
        def _():
            put_wide(w_out.at[layer], c * half, (u - at_out) * WIDE, slot)

        @pl.when(block & (u >= at_up) & (u < at_down))
        def _():
            put_deep(w_up.at[layer], c * hidden + (u - at_up) * TILE, slot)

        @pl.when(block & (u >= at_down))
        def _():
            d = u - at_down
            put_wide(w_down.at[layer], c * hidden + lax.rem(d, n_deep) * half, lax.div(d, n_deep) * WIDE, slot)

        @pl.when(live & (inside >= LAYERS * n_block))
        def _():
            put_deep(w_head, c * half + (inside - LAYERS * n_block) * TILE, slot)

    def tile_loop(base, count, body, hooks=()):
        def one(t, carry):
            n = base + t
            slot = lax.rem(n, n_buf)
            tile = wbuf.at[slot]
            pltpu.make_async_copy(tile, tile, w_sem.at[slot]).wait()
            body(t, tile)
            issue(n + n_buf)
            for at, when, hook in hooks:
                pl.when((t == at) & when)(hook)
            return carry

        lax.fori_loop(0, count, one, 0)

    def deep_dot(tile):
        return dot(h[:, :half], tile[:, :TILE]) + dot(h[:, half:], tile[:, TILE:])

    def load_kv(old_k, old_v):
        for i, src in ((K, old_k), (V, old_v)):
            pltpu.make_async_copy(src, (kbuf, vbuf)[i], kv_sem.at[i]).start()

    def load_stale(b):
        columns = pl.ds(pl.multiple_of(z * group, group), group)
        load_kv(k_old.at[b, :, :, :, :, columns], v_old.at[b, :, :, :, :, columns])

    def load_shared(b):
        load_kv(shared.at[b, K], shared.at[b, V])

    share = [
        [share_rings(shared.at[b, i], color, torus, share_send.at[b, i, color], share_recv.at[b, i, color]) for i in (K, V) for color in range(2)]
        for b in range(LAYERS)
    ]
    full = [
        [
            [full_rings((all_k, all_v)[i].at[b], color, torus, full_send.at[b, i, color], full_recv.at[b, i, color]) for color in range(3)]
            for i in (K, V)
        ]
        for b in range(LAYERS)
    ]

    def first(rings, k):
        for ring in rings:
            if k:
                ring[k - 1].settle()
            ring[k].first()

    def relay(rings, k):
        for ring in rings:
            ring[k].relay()

    def settle(rings, k):
        for ring in rings:
            ring[k].settle()

    barrier = pltpu.get_barrier_semaphore()

    def announce(**device_id):
        pl.semaphore_signal(barrier, inc=1, device_id=device_id, device_id_type=MESH)

    for i in range(n_ada):
        issue_ada(i)
    announce(cfg=other)
    for by in range(1, RING):
        for core in range(2):
            announce(patch=torus.patch["z", by], cfg=core)
        announce(patch=torus.patch["y", by])
        announce(patch=torus.patch["x", by])
    pl.semaphore_wait(barrier, 1 + 4 * (RING - 1))

    cond_swap = remote(cond, cond_peer, cond_sem.at[0], cond_sem.at[1], cfg=other)
    cond_swap.start()
    xs[0] = lat[...].astype(F32)
    cond_swap.wait()
    mine, theirs = cond[...], cond_peer[...]
    both = jnp.concatenate([jnp.where(c == 0, mine, theirs), jnp.where(c == 0, theirs, mine)], axis=0)
    silu = (both * jax.nn.sigmoid(both)).astype(BF16)
    for i in range(n_ada):
        filled = wbuf.at[i, :, pl.ds(0, 2 * chunk)]
        pltpu.make_async_copy(filled, filled, w_sem.at[i]).wait()
    for n in range(n_ada, n_buf):
        issue(jnp.int32(n))
    load_stale(0)
    for i in range(n_ada):
        tile = wbuf.at[i]
        mod[c, y, x, :, pl.ds(i * chunk, chunk)] = dot(silu[:, :half], tile[:, :chunk]) + dot(silu[:, half:], tile[:, chunk : 2 * chunk])
        issue(jnp.int32(n_buf + i))
    mod_copies = []
    for axis, part in (("y", mod.at[c, y, x]), ("x", mod.at[c, :, x])):
        stage = []
        for by in range(1, RING):
            slot = len(mod_copies) + len(stage)
            stage.append(remote(part, part, mod_send.at[slot], mod_recv.at[slot], patch=torus.patch[axis, by]))
        for one in stage:
            one.start()
        for one in stage:
            one.wait_recv()
        mod_copies += stage
    mod_swap = remote(mod.at[c], mod.at[c], mod_send.at[len(mod_copies)], mod_recv.at[len(mod_copies)], cfg=other)
    mod_swap.start()
    mod_swap.wait_recv()
    mod_copies.append(mod_swap)

    def mod_row(b, step, which, i, s):
        piece = which * 8 + i
        at = piece // n_ada
        columns = slice((piece % n_ada) * chunk, (piece % n_ada + 1) * chunk)
        both = mod[b, at // RING, at % RING, s * STEPS : (s + 1) * STEPS, columns]
        return jnp.where(step == 0, both[0:1], both[1:2])

    def normed(s):
        values = r[s * rows : (s + 1) * rows, :]
        centered = values - jnp.mean(values, -1, keepdims=True)
        return centered * lax.rsqrt(jnp.mean(centered * centered, -1, keepdims=True) + 1e-6)

    def modulate(b, step, shift, gain):
        for s in range(2):
            values = normed(s)
            for i in range(8):
                at = slice(i * chunk, (i + 1) * chunk)
                part = values[:, at] * (1.0 + mod_row(b, step, gain, i, s)) + mod_row(b, step, shift, i, s)
                h[s * rows : (s + 1) * rows, at] = part.astype(BF16)

    def add_gated(b, step, gate, own, peer):
        for s in range(2):
            for i in range(8):
                at = (slice(s * rows, (s + 1) * rows), slice(i * chunk, (i + 1) * chunk))
                r[at] = r[at] + mod_row(b, step, gate, i, s) * (own[at] + peer[at])

    def chunk_swap(own, peer, t, send_sem, recv_sem):
        columns = pl.ds(pl.multiple_of(t * WIDE, WIDE), WIDE)
        return remote(own.at[:, columns], peer.at[:, columns], send_sem.at[t], recv_sem.at[t], cfg=other)

    def qkv_copy(p, s, g):
        return remote(sb.at[s, g, p], rb.at[p, z], qkv_send.at[p, s, g], qkv_recv.at[p, z], patch=pair_patch[g], cfg=s)

    def qkv_out(p, do_send):
        for s in range(2):
            for g in range(2):
                here = (2 * c + g == z) & (c == s)
                away = (2 * c + g != z) | (c != s)
                if do_send:

                    @pl.when(here)
                    def _():
                        rb[p, z] = sb[s, g, p]

                    @pl.when(away)
                    def _():
                        qkv_copy(p, s, g).start()
                else:

                    @pl.when(away)
                    def _():
                        qkv_copy(p, s, g).wait_send()

    def qkv_in(p):
        for src in range(RING):

            @pl.when((z != src) | (c != z_core))
            def _():
                part = rb.at[p, src]
                remote(part, part, qkv_send.at[p, 0, 0], qkv_recv.at[p, src], cfg=other).wait_recv()

    def qkv_part(p, base):
        def body(t, tile):
            part = deep_dot(tile).astype(BF16)
            for k in range(TILE // SUB):
                col = t * TILE + k * SUB
                g = lax.div(col, group)
                columns = pl.ds(pl.multiple_of(col - g * group, SUB), SUB)
                for s in range(2):
                    sb[s, g, p, :, columns] = part[s * rows : (s + 1) * rows, k * SUB : (k + 1) * SUB]

        tile_loop(base + p * n_qkv, n_qkv, body)
        qkv_out(p, True)

    def own_copies(b, i):
        local, swap = [], []
        for g in range(2):
            columns = pl.ds(pl.multiple_of(c * half + g * group, group), group)
            place = (all_k, all_v)[i].at[b, z, y, x, :, columns]
            local.append(pltpu.make_async_copy(sb.at[c, g, i], place, own_put.at[i, g]))
            swap.append(remote(sb.at[other, g, i], place, own_send.at[i, g], own_recv.at[i, g], cfg=other))
        return local, swap

    def own_start(b, i):
        local, swap = own_copies(b, i)
        for one in local + swap:
            one.start()

    def own_wait(b, i):
        local, swap = own_copies(b, i)
        for one in local + swap:
            one.wait()

    def share_copy(b, i):
        return pltpu.make_async_copy(rb.at[i], shared.at[b, i, :, y, x], share_put.at[i])

    tokens_z = RING * RING * rows
    n_rows = RING * rows

    def attention(hooks):
        def patch_of(index):
            return lax.div(index, jnp.full_like(index, rows))

        row_z = patch_of(lax.broadcasted_iota(jnp.int32, (n_rows, tokens_z), 0))
        col_p = patch_of(lax.broadcasted_iota(jnp.int32, (n_rows, tokens_z), 1))
        row_f = patch_of(lax.broadcasted_iota(jnp.int32, (n_rows, n_rows), 0))
        col_f = patch_of(lax.broadcasted_iota(jnp.int32, (n_rows, n_rows), 1))

        def scored(queries, keys):
            return lax.dot_general(queries, keys, (((1,), (1,)), ((), ())), preferred_element_type=F32)

        def one(head, carry):
            at = pl.ds(pl.multiple_of(head * HEAD, HEAD), HEAD)
            queries = rb[Q, :, :, at].reshape(n_rows, HEAD)
            fresh = scored(queries, rb[K, :, :, at].reshape(n_rows, HEAD))
            fresh = jnp.where(row_f == col_f, fresh, -jnp.inf)
            top = jnp.max(fresh, -1, keepdims=True)
            for plane in range(RING):
                part = scored(queries, kbuf[plane, :, :, :, at].reshape(tokens_z, HEAD))
                part = jnp.where((row_z == plane) & (col_p == y * RING + x), -jnp.inf, part)
                scores[:, plane * tokens_z : (plane + 1) * tokens_z] = part
                top = jnp.maximum(top, jnp.max(part, -1, keepdims=True))
            weights = jnp.exp((fresh - top) * scale)
            total = jnp.sum(weights, -1, keepdims=True)
            mixed = dot(weights.astype(BF16), rb[V, :, :, at].reshape(n_rows, HEAD))
            for plane in range(RING):
                weights = jnp.exp((scores[:, plane * tokens_z : (plane + 1) * tokens_z] - top) * scale)
                total = total + jnp.sum(weights, -1, keepdims=True)
                mixed = mixed + dot(weights.astype(BF16), vbuf[plane, :, :, :, at].reshape(tokens_z, HEAD))
            o_own[:, :, at] = (mixed / total).astype(BF16).reshape(RING, rows, HEAD)
            for at, when, hook in hooks:
                pl.when((head == at) & when)(hook)
            return carry

        for i in (K, V):
            buf = (kbuf, vbuf)[i]
            pltpu.make_async_copy(buf, buf, kv_sem.at[i]).wait()
        lax.fori_loop(0, group // HEAD, one, 0)

    def o_copy(dst):
        return remote(o_own.at[dst], ob.at[c, z_odd], o_send.at[dst], o_recv.at[c, z_odd], patch=z_patch[dst], cfg=z_core)

    def o_out(do_send):
        for dst in range(RING):
            if do_send:

                @pl.when((z == dst) & (c == z_core))
                def _():
                    ob[c, z_odd] = o_own[dst]

            @pl.when((z != dst) | (c != z_core))
            def _():
                if do_send:
                    o_copy(dst).start()
                else:
                    o_copy(dst).wait_send()

    def o_in():
        for s in range(2):
            for g in range(2):

                @pl.when((2 * c + g != z) | (c != s))
                def _():
                    part = ob.at[s, g]
                    remote(part, part, o_send.at[0], o_recv.at[s, g], cfg=other).wait_recv()

    def block(step, b):
        base = n_ada + step * n_step + b * n_block
        begin = step == 0
        last = step == STEPS - 1
        heads = group // HEAD
        no_hooks = ()

        def unless_first(action):
            if b:
                action()
            else:
                pl.when(step > 0)(action)

        if b == 0:
            for s in range(2):
                r[s * rows : (s + 1) * rows, :] = xs[step]
        modulate(b, step, 0, 1)

        @unless_first
        def _():
            for p in (K, V, Q):
                qkv_out(p, False)

        qkv_part(K, base)

        @pl.when(last)
        def _():
            own_start(b, K)

        qkv_part(V, base)

        @pl.when(last)
        def _():
            own_start(b, V)
            own_wait(b, K)
            first(full[b][K], 0)

        @pl.when(begin if b else last)
        def _():
            relay(share[1 - b], 1)

        qkv_part(Q, base)

        @pl.when(last)
        def _():
            own_wait(b, V)
            first(full[b][V], 0)
            if b:
                first(full[0][V], 2)

        for p in (K, V, Q):
            qkv_in(p)

        @pl.when(begin)
        def _():
            for p in (K, V):
                share_copy(b, p).start()

        @unless_first
        def _():
            o_out(False)

        if b:
            hooks = ((heads - 1, last, lambda: relay(full[0][K], 2)),)
        else:
            hooks = ((heads // 3, last, lambda: relay(full[0][K], 0)), (heads - 1, last, lambda: relay(full[0][V], 0)))
        attention(hooks)

        @pl.when(begin)
        def _():
            for p in (K, V):
                share_copy(b, p).wait()

        o_out(True)

        @pl.when(begin)
        def _():
            if b == 0:
                load_stale(1)
            first(share[b], 0)

        @pl.when(last)
        def _():
            if b == 0:
                first(full[0][K], 1)
            else:
                relay(full[1][K], 0)
                relay(full[1][V], 0)

        o_in()

        def out_body(t, tile):
            columns = pl.ds(pl.multiple_of(t * WIDE, WIDE), WIDE)
            part = [ob[:, g].reshape(2 * rows, group) for g in range(2)]
            out_own[:, columns] = dot(part[0], tile[:group]) + dot(part[1], tile[group:])
            chunk_swap(out_own, out_peer, t, out_send, out_recv).start()

        @unless_first
        def _():
            for t in range(n_out):
                chunk_swap(out_own, out_peer, t, out_send, out_recv).wait_send()

        tile_loop(base + 3 * n_qkv, n_out, out_body)
        if b == 0:

            @pl.when(last)
            def _():
                first(full[0][V], 1)

        for t in range(n_out):
            chunk_swap(out_own, out_peer, t, out_send, out_recv).wait_recv()
        add_gated(b, step, 2, out_own, out_peer)
        modulate(b, step, 3, 4)

        def up_body(t, tile):
            act[:, pl.ds(pl.multiple_of(t * TILE, TILE), TILE)] = jax.nn.gelu(deep_dot(tile), approximate=True).astype(BF16)

        def refill(share_in, then):
            settle(share_in, 1)
            load_shared(1 - b)
            then()

        if b:
            hooks = (
                (1, begin, lambda: refill(share[0], lambda: relay(share[1], 0))),
                (n_up // 2, begin, lambda: first(share[1], 1)),
            )
        else:
            hooks = (
                (1, begin, lambda: relay(share[0], 0)),
                (n_up // 2, begin, lambda: first(share[0], 1)),
                (1, last, lambda: refill(share[1], lambda: None)),
                (n_up // 2 - 1, last, lambda: relay(full[0][K], 1)),
                (n_up * 3 // 4, last, lambda: relay(full[0][V], 1)),
            )
        tile_loop(base + 3 * n_qkv + n_out, n_up, up_body, hooks)

        def down_body(t, tile):
            n = lax.div(t, n_deep)
            deep = lax.rem(t, n_deep)
            columns = pl.ds(pl.multiple_of(n * WIDE, WIDE), WIDE)
            part = dot(act[:, pl.ds(pl.multiple_of(deep * half, half), half)], tile[...])

            @pl.when(deep == 0)
            def _():
                down_own[:, columns] = part

            @pl.when(deep != 0)
            def _():
                down_own[:, columns] = down_own[:, columns] + part

            @pl.when(deep == n_deep - 1)
            def _():
                chunk_swap(down_own, down_peer, n, down_send, down_recv).start()

        @unless_first
        def _():
            for t in range(n_out):
                chunk_swap(down_own, down_peer, t, down_send, down_recv).wait_send()

        if b:
            hooks = (
                (n_down // 2, last, lambda: first(full[1][K] + full[1][V], 1)),
                (n_down - 1, last, lambda: relay(full[0][V], 2)),
            )
        else:
            hooks = ((0, last, lambda: first(full[0][K], 2)),)
        tile_loop(base + 3 * n_qkv + n_out + n_up, n_down, down_body, hooks)
        for t in range(n_out):
            chunk_swap(down_own, down_peer, t, down_send, down_recv).wait_recv()
        add_gated(b, step, 5, down_own, down_peer)

    def one_step(step, carry):
        for b in range(LAYERS):
            block(step, b)
        for s in range(2):
            h[s * rows : (s + 1) * rows, :] = normed(s).astype(BF16)
        later = lax.rem(step + 1, STEPS)

        def head_body(t, tile):
            eps = deep_dot(tile).astype(BF16).astype(F32)
            with_cond, without = eps[:rows], eps[rows:]
            guided = without + sched[2, step] * (with_cond - without)
            columns = pl.ds(pl.multiple_of(c * half + t * TILE, TILE), TILE)
            xs[later, :, columns] = sched[0, step] * xs[step, :, columns] + sched[1, step] * guided

        @pl.when(step > 0)
        def _():
            x_half(xs, step, c, half, x_sem, other).wait_send()

        tile_loop(n_ada + step * n_step + LAYERS * n_block, n_head, head_body)
        swap = x_half(xs, later, c, half, x_sem, other)
        swap.start()
        swap.wait_recv()
        return carry

    lax.fori_loop(0, STEPS, one_step, 0)
    lat_out[...] = xs[0]

    for i in (K, V):
        relay(full[1][i], 1)
    for i in (K, V):
        first(full[1][i], 2)
    for i in (K, V):
        relay(full[1][i], 2)
    for b in range(LAYERS):
        for i in (K, V):
            settle(full[b][i], 2)
    x_half(xs, 0, c, half, x_sem, other).wait_send()
    for p in (K, V, Q):
        qkv_out(p, False)
    o_out(False)
    for t in range(n_out):
        chunk_swap(out_own, out_peer, t, out_send, out_recv).wait_send()
        chunk_swap(down_own, down_peer, t, down_send, down_recv).wait_send()
    for one in mod_copies:
        one.wait_send()
    for b in range(LAYERS):
        for ring in share[b] + full[b][K] + full[b][V]:
            for stage in ring:
                stage.drain()


def x_half(xs, at, c, half, x_sem, other):
    part = xs.at[at, :, pl.ds(pl.multiple_of(c * half, half), half)]
    return remote(part, part, x_sem.at[0], x_sem.at[1], cfg=other)


def denoise(lat, cond, sched, w_ada, w_qkv, w_out, w_up, w_down, w_head, k_old, v_old):
    rows, width = lat.shape
    group = width // RING
    hidden = w_up.shape[2] // 2
    torus = (RING, RING, RING)
    cache = jax.ShapeDtypeStruct((LAYERS, *torus, rows, width), BF16)
    k_old = k_old.reshape(cache.shape)
    v_old = v_old.reshape(cache.shape)
    w_out = w_out.reshape(LAYERS, width, width)
    n_out = width // WIDE
    anywhere = pl.BlockSpec(memory_space=pl.ANY)
    vmem = pl.BlockSpec(memory_space=pltpu.VMEM)
    dma = pltpu.SemaphoreType.DMA
    lat_out, all_k, all_v, _ = pl.pallas_call(
        denoise_kernel,
        out_shape=(
            jax.ShapeDtypeStruct((rows, width), F32),
            cache,
            cache,
            jax.ShapeDtypeStruct((LAYERS, 2, *torus, rows, group), BF16),
        ),
        in_specs=[vmem, vmem, pl.BlockSpec(memory_space=pltpu.SMEM)] + [anywhere] * 8,
        out_specs=[vmem, anywhere, anywhere, anywhere],
        scratch_shapes=[
            pltpu.VMEM((BUFFERS, width // 2, WIDE), BF16),
            pltpu.VMEM((*torus, rows, group), BF16),
            pltpu.VMEM((*torus, rows, group), BF16),
            pltpu.VMEM((STEPS, rows, width), F32),
            pltpu.VMEM((2 * rows, width), F32),
            pltpu.VMEM((2 * rows, width), BF16),
            pltpu.VMEM((2 * rows, hidden), BF16),
            pltpu.VMEM((2 * rows, width), F32),
            pltpu.VMEM((2 * rows, width), F32),
            pltpu.VMEM((2 * rows, width), F32),
            pltpu.VMEM((2 * rows, width), F32),
            pltpu.VMEM((2, 2, 3, rows, group), BF16),
            pltpu.VMEM((3, RING, rows, group), BF16),
            pltpu.VMEM((RING, rows, group), BF16),
            pltpu.VMEM((2, 2, rows, group), BF16),
            pltpu.VMEM((LAYERS, RING, RING, 2 * STEPS, 3 * width // 8), F32),
            pltpu.VMEM((STEPS, width), F32),
            pltpu.VMEM((RING * rows, RING**3 * rows), F32),
            dma((BUFFERS,)),
            dma((2,)),
            dma((2,)),
            dma((2 * RING - 1,)),
            dma((2 * RING - 1,)),
            dma((3, 2, 2)),
            dma((3, RING)),
            dma((RING,)),
            dma((2, 2)),
            dma((n_out,)),
            dma((n_out,)),
            dma((n_out,)),
            dma((n_out,)),
            dma((2,)),
            dma((2,)),
            dma((LAYERS, 2, 2, 2, 4)),
            dma((LAYERS, 2, 2, 2, 4)),
            dma((2, 2)),
            dma((2, 2)),
            dma((2, 2)),
            dma((LAYERS, 2, 3, 3, 4)),
            dma((LAYERS, 2, 3, 3, 4)),
        ],
        compiler_params=pltpu.CompilerParams(collective_id=0, has_side_effects=True, vmem_limit_bytes=63 * 2**20),
        name="denoise",
    )(lat, cond, sched, w_ada, w_qkv, w_out, w_up, w_down, w_head, k_old, v_old)
    tokens = RING**3 * rows
    return lat_out, all_k.reshape(LAYERS, tokens, width), all_v.reshape(LAYERS, tokens, width)


def solution(mesh):
    slot_spec = P(("img", "cfg"), None, None)
    cache_spec = P(("img", "cfg"), None, None, None)
    rep_spec = P()

    def local_step(latent, cond_vec, sched_coef, w_ada, w_qkv, w_out, w_up, w_down, w_head, k_stale, v_stale):
        lat_out, k_new, v_new = denoise(
            latent[0], cond_vec[0], sched_coef, w_ada, w_qkv, w_out, w_up, w_down, w_head, k_stale[0], v_stale[0]
        )
        return lat_out[None], k_new[None], v_new[None]

    return jax.shard_map(
        local_step,
        mesh=mesh,
        in_specs=(P("img", "patch", None), slot_spec, rep_spec, rep_spec, rep_spec, rep_spec, rep_spec, rep_spec, rep_spec, cache_spec, cache_spec),
        out_specs=(P(("img", "cfg"), "patch", None), cache_spec, cache_spec),
        check_vma=False,
    )
```

time: 914 us -> 381 us (0.42)
  matrix products: 476 us -> 0 us
  Pallas kernels: 0 us -> 344 us
  waiting for transfers between devices: 243 us -> 0 us
  local copies, waits for them, and re-layouts: 116 us -> 36.3 us
  other arithmetic: 54.2 us -> 0.01 us
  between operations: 14.9 us -> 0.7 us
    dot_general x23 -> x0, matrix products: 476 us -> none  [the longest x4 107 us: local_step(): jnp.dot(norm_mlp, w_up[layer_idx], preferred_element_type=jnp.float32)]
    pallas_call x0 -> x1, Pallas kernels: none -> 344 us  [denoise(): pl.pallas_call(denoise_kernel, out_shape=(jax.ShapeDtypeStruct((rows, wid...]
    all_gather x8 -> x0, waiting for transfers between devices: 238 us -> none  [the longest x4 166 us: local_step(): v_next.append(lax.all_gather(v_new, 'patch', axis=0, tiled=True))]
    reshape x4 -> x0, local copies, waits for them, and re-layouts: 66.4 us -> none  [attend(): val_h = value_set.reshape(tokens, n_heads, head_dim)]
    broadcast_in_dim x3 -> x0, other arithmetic: 43.8 us -> none  [the longest x1 20.5 us: local_step(): jnp.stack(k_cache)[None]]
    squeeze x1 -> x0, local copies, waits for them, and re-layouts: 33.9 us -> none  [local_step(): k_cache = [k_stale[0, layer_idx] for layer_idx in range(n_layers)]]
    unnamed x42 -> x16, local copies, waits for them, and re-layouts: 10.9 us -> 36.3 us
    reduce_sum x16 -> x0, other arithmetic: 9.29 us -> none  [the longest x4 4.67 us: one_block(): row_sum = jnp.sum(weights, -1)]
  transfers between devices with their start and end apart: 10 -> 0, of which waited for: 6 -> 0; matrix products, arithmetic and copies ran while one was open for 54% -> 0% of each run, Pallas kernels for 0% -> 0%
where the time goes in v2:
time: 381 us
  Pallas kernels  344 us (90%)
  local copies, waits for them, and re-layouts  36.3 us (10%)
    pallas_call x1, Pallas kernels, denoise(): pl.pallas_call(denoise_kernel, out_shape=(jax.ShapeDtypeStruct((rows, wid...  344 us
    unnamed x16, local copies, waits for them, and re-layouts  36.3 us

profile of v2, /device:TPU:1, one launch (start us, length us, event | category | flops | bytes accessed | tf_op | source)
XLA Modules:
  0.0 381.1 jit_solution(12040418902770787258)
XLA Ops:
  0.6 1.3 copy.14.sched
  2.0 344.1 %denoise.1 = (f32[32,3072]{1,0:T(8,128)}, bf16[2,4,4,4,32,3072]{5,4,3,2,1,0:T(8,128)(2,1)}, bf16[2,4,4,4,32,3072]{5,4,3,2,1,0:T(8,128)(2,1)}, bf16[2,2,4,4,4,32,768]{6,5,4,3,2,1,0:T(8,128)(2,1)}) custom-call(bf16[32,3072]{1,0:T(8,128)(2,1)} %bitcast.16, f32[2,3072]{1,0:T(2,128)} %bitcast.17, f32[3,2]{1,0:T(4,128)} %copy.14.sched, ...), custom_call_target="tpu_custom_call" | custom-call | tf_op jit(solution)/shard_map/denoise/pallas_call | solution.py:719
  346.1 0.0 slice-start
  346.1 1.9 copy.18
  348.0 0.0 slice-start.1
  348.0 0.0 slice-start.2
  348.0 0.0 slice-start.3
  348.0 0.0 slice-start.4
  348.0 0.0 slice-start.5
  348.0 24.1 %copy.19 = bf16[1,2,2048,3072]{3,2,1,0:T(8,128)(2,1)} copy(bf16[1,2,2048,3072]{3,2,1,0:T(8,128)(2,1)} %bitcast.14) | data formatting | bytes 50331648
  372.1 0.0 slice-done
  372.1 0.0 slice-done.1
  372.1 0.0 slice-done.2
  372.1 0.0 slice-done.3
  372.1 0.0 slice-done.4
  372.1 0.0 slice-done.5
  372.1 8.9 %copy.20 = bf16[1,2,2048,3072]{3,2,1,0:T(8,128)(2,1)} copy(bf16[1,2,2048,3072]{3,2,1,0:T(8,128)(2,1)S(1)} %bitcast.13) | data formatting | bytes 50331648
  (1 shorter events, 0.0 us)
Async XLA Ops:
  346.1 26.0 %slice-start = ((s8[25165824]{0:T(1024)(128)(4,1)}), s8[4194304]{0:T(1024)(128)(4,1)S(1)}, s32[]{:S(2)}) async-start(s8[25165824]{0:T(1024)(128)(4,1)} %bitcast.11), calls=%async_computation | async-start | bytes 8388608
  348.0 24.1 %slice-start.1 = ((s8[25165824]{0:T(1024)(128)(4,1)}), s8[4194304]{0:T(1024)(128)(4,1)S(1)}, s32[]{:S(2)}) async-start(s8[25165824]{0:T(1024)(128)(4,1)} %bitcast.11), calls=%async_computation.1 | async-start | bytes 8388608
  348.0 24.1 %slice-start.2 = ((s8[25165824]{0:T(1024)(128)(4,1)}), s8[4194304]{0:T(1024)(128)(4,1)S(1)}, s32[]{:S(2)}) async-start(s8[25165824]{0:T(1024)(128)(4,1)} %bitcast.11), calls=%async_computation.2 | async-start | bytes 8388608
  348.0 24.1 %slice-start.3 = ((s8[25165824]{0:T(1024)(128)(4,1)}), s8[4194304]{0:T(1024)(128)(4,1)S(1)}, s32[]{:S(2)}) async-start(s8[25165824]{0:T(1024)(128)(4,1)} %bitcast.11), calls=%async_computation.3 | async-start | bytes 8388608
  348.0 24.1 %slice-start.4 = ((s8[25165824]{0:T(1024)(128)(4,1)}), s8[4194304]{0:T(1024)(128)(4,1)S(1)}, s32[]{:S(2)}) async-start(s8[25165824]{0:T(1024)(128)(4,1)} %bitcast.11), calls=%async_computation.4 | async-start | bytes 8388608
  348.0 24.1 %slice-start.5 = ((s8[25165824]{0:T(1024)(128)(4,1)}), s8[4194304]{0:T(1024)(128)(4,1)S(1)}, s32[]{:S(2)}) async-start(s8[25165824]{0:T(1024)(128)(4,1)} %bitcast.11), calls=%async_computation.5 | async-start | bytes 8388608
